TPU v7x, 16 devices: a whole 2x2x2 slice. The times are simulated.
16 devices in a mesh: dp: 4 (over z, y), sp: 4 (over x, core).
Axes of the slice: x: 2, y: 2, z: 2, core: 2. Of those that a mesh axis runs over, the one named last changes fastest.
Arguments:
- resid_x: bfloat16 [48, 512, 5120], P('dp', 'sp'), parts along dimension 0
- positions: int32 [48, 512], P('dp', 'sp'), parts along dimension 0
- w_query: bfloat16 [5120, 5120], replicated
- w_key: bfloat16 [5120, 5120], replicated
- w_value: bfloat16 [5120, 5120], replicated
- w_out: bfloat16 [5120, 5120], replicated
- gain_q: bfloat16 [5120], replicated
- gain_k: bfloat16 [5120], replicated
- gain_out: bfloat16 [5120], replicated
Outputs:
- output: bfloat16 [48, 512, 5120], P('dp', 'sp'), parts along dimension 0
There are 4 independent parts. A program takes and returns all parts, laid end to end along the dimension named above; an argument that names none is the same for every part.
All inputs are finite; a program needn't handle non-finite values.
Results may differ from a plain program's by a relative error of at most 0.0172881.
Values are sent between devices in bfloat16 or wider.
A program may use at most 1 GiB of HBM per device.

v0:
```python
import jax
import jax.numpy as jnp
from jax import lax
from jax.sharding import PartitionSpec as P

HEAD_DIM = 128
QUERY_BLOCKS = 8
ROPE_THETA = 500000.0
NORM_EPS = 1e-6
SCALE = HEAD_DIM ** -0.5


def rope_tables(pos_ids):
    inv_freq = 1.0 / (ROPE_THETA ** (jnp.arange(0, HEAD_DIM, 2, dtype=jnp.float32) / HEAD_DIM))
    angles = pos_ids.astype(jnp.float32)[..., None] * inv_freq
    return jnp.cos(angles), jnp.sin(angles)


def apply_rope(heads_f32, cos_t, sin_t):
    half = HEAD_DIM // 2
    cos_b = cos_t[:, :, None, :]
    sin_b = sin_t[:, :, None, :]
    first = heads_f32[..., :half]
    second = heads_f32[..., half:]
    return jnp.concatenate([first * cos_b - second * sin_b, second * cos_b + first * sin_b], axis=-1)


def rms_scale(vals_f32, gain):
    mean_sq = jnp.mean(vals_f32 * vals_f32, axis=-1, keepdims=True)
    return vals_f32 * lax.rsqrt(mean_sq + NORM_EPS) * gain.astype(jnp.float32)


def project(x_tok, weight):
    return jnp.einsum('bsd,de->bse', x_tok, weight, preferred_element_type=jnp.float32).astype(jnp.bfloat16)


def norm_rope(x_tok, weight, gain, cos_t, sin_t):
    proj = project(x_tok, weight).astype(jnp.float32)
    batch, seq_len, model_width = proj.shape
    normed = rms_scale(proj, gain).reshape(batch, seq_len, model_width // HEAD_DIM, HEAD_DIM)
    return apply_rope(normed, cos_t, sin_t).astype(jnp.bfloat16)


def causal_attention(q_heads, k_heads, v_heads):
    seq_len = q_heads.shape[1]
    block = seq_len // QUERY_BLOCKS
    outs = []
    for blk_idx in range(QUERY_BLOCKS):
        key_end = (blk_idx + 1) * block
        q_blk = q_heads[:, blk_idx * block:key_end]
        scores = jnp.einsum('bqhd,bkhd->bhqk', q_blk, k_heads[:, :key_end], preferred_element_type=jnp.float32) * SCALE
        q_idx = blk_idx * block + jnp.arange(block)
        scores = jnp.where(jnp.arange(key_end)[None, :] <= q_idx[:, None], scores, -1e30)
        probs = jax.nn.softmax(scores, axis=-1).astype(jnp.bfloat16)
        outs.append(jnp.einsum('bhqk,bkhd->bqhd', probs, v_heads[:, :key_end], preferred_element_type=jnp.float32).astype(jnp.bfloat16))
    return jnp.concatenate(outs, axis=1)


def solution(mesh):
    def local_block(x_loc, pos_loc, w_query, w_key, w_value, w_out, gain_q, gain_k, gain_out):
        batch, seq_loc, model_width = x_loc.shape
        cos_t, sin_t = rope_tables(pos_loc)
        q_loc = norm_rope(x_loc, w_query, gain_q, cos_t, sin_t)
        k_loc = norm_rope(x_loc, w_key, gain_k, cos_t, sin_t)
        v_loc = project(x_loc, w_value).reshape(batch, seq_loc, model_width // HEAD_DIM, HEAD_DIM)
        q_heads = lax.all_to_all(q_loc, 'sp', 2, 1, tiled=True)
        k_heads = lax.all_to_all(k_loc, 'sp', 2, 1, tiled=True)
        v_heads = lax.all_to_all(v_loc, 'sp', 2, 1, tiled=True)
        o_heads = causal_attention(q_heads, k_heads, v_heads)
        o_loc = lax.all_to_all(o_heads, 'sp', 1, 2, tiled=True).reshape(batch, seq_loc, model_width)
        attn_out = project(o_loc, w_out).astype(jnp.float32)
        return (x_loc.astype(jnp.float32) + rms_scale(attn_out, gain_out)).astype(jnp.bfloat16)

    tok_spec = P('dp', 'sp', None)
    return jax.shard_map(local_block, mesh=mesh, in_specs=(tok_spec, P('dp', 'sp'), P(), P(), P(), P(), P(), P(), P()), out_specs=tok_spec, check_vma=False)
```

profile of v0, /device:TPU:0, one launch (start us, length us, event | category | flops | bytes accessed | tf_op | source)
XLA Modules:
  0.0 1483.9 jit_solution(2167946907499969882)
XLA Ops:
  0.0 0.5 negate_power_fusion
  0.5 91.2 %fusion.18 = (f32[12,128]{1,0:T(8,128)S(1)}, bf16[12,128,5120]{2,1,0:T(8,128)(2,1)}) fusion(bf16[12,128,5120]{2,1,0:T(8,128)(2,1)} %param.9, bf16[5120,5120]{1,0:T(8,128)(2,1)} %param.12), kind=kOutput, calls=%fused_computation.24 | convolution fusion | flops 80562094080 | bytes 83892224 | tf_op jit(solution)/shard_map/bsd,de->bse/dot_general | solution.py:34
  91.7 9.5 fusion.19
  101.3 11.9 copy.84
  113.2 91.8 %fusion.16 = (f32[12,128]{1,0:T(8,128)S(1)}, bf16[12,128,5120]{2,1,0:T(8,128)(2,1)}) fusion(bf16[12,128,5120]{2,1,0:T(8,128)(2,1)} %param.9, bf16[5120,5120]{1,0:T(8,128)(2,1)} %param.11), kind=kOutput, calls=%fused_computation.22 | convolution fusion | flops 80562094080 | bytes 83892224 | tf_op jit(solution)/shard_map/bsd,de->bse/dot_general | solution.py:34
  205.0 0.0 copy-done.4
  205.0 9.5 fusion.17
  214.6 0.0 copy-start.6
  214.6 11.9 copy.83
  226.4 79.7 %fusion.146 = (f32[12,128,40,64]{3,2,1,0:T(8,128)}, f32[12,128,40,64]{3,2,1,0:T(8,128)}, f32[12,128,40,64]{3,2,1,0:T(8,128)}, f32[12,128,40,64]{3,2,1,0:T(8,128)}) fusion(f32[12,128,40,128]{3,2,1,0:T(8,128)} %bitcast.87, f32[12,128,40,128]{3,2,1,0:T(8,128)} %bitcast.86), kind=kLoop, calls=%fused_computation.186 | loop fusion | bytes 125829120 | tf_op jit(solution)/shard_map/slice | solution.py:23
  306.2 2.8 multiply_cosine_fusion
  309.0 72.7 %subtract_convert_fusion.1 = (bf16[12,128,40,64]{3,1,0,2:T(8,128)(2,1)}, bf16[12,128,40,64]{3,1,0,2:T(8,128)(2,1)}, bf16[12,128,40,64]{3,1,0,2:T(8,128)(2,1)}, bf16[12,128,40,64]{3,1,0,2:T(8,128)(2,1)}) fusion(f32[12,128,40,64]{3,2,1,0:T(8,128)} %get-tuple-element.10, f32[12,128,40,64]{3,2,1,0:T(8,128)} %get-tuple-element.9, ...), kind=kLoop, calls=%fused_computation.33 | loop fusion | flops 62914560 | bytes 95158272 | tf_op jit(solution)/shard_map/convert.2
  381.7 19.8 %pad_maximum_fusion = bf16[12,128,40,128]{3,1,0,2:T(8,128)(2,1)} fusion(bf16[12,128,40,64]{3,1,0,2:T(8,128)(2,1)} %get-tuple-element.6, bf16[12,128,40,64]{3,1,0,2:T(8,128)(2,1)} %get-tuple-element.5), kind=kLoop, calls=%fused_computation.35 | loop fusion | flops 31457280 | bytes 31457280 | tf_op jit(solution)/shard_map/concatenate | solution.py:25
  401.6 7.2 all-to-all-start.1
  408.8 19.8 %pad_maximum_fusion.1 = bf16[12,128,40,128]{3,1,0,2:T(8,128)(2,1)} fusion(bf16[12,128,40,64]{3,1,0,2:T(8,128)(2,1)} %get-tuple-element.13, bf16[12,128,40,64]{3,1,0,2:T(8,128)(2,1)} %get-tuple-element.14), kind=kLoop, calls=%fused_computation.36 | loop fusion | flops 31457280 | bytes 31457280 | tf_op jit(solution)/shard_map/concatenate | solution.py:25
  428.6 152.7 %all-to-all-done.1 = bf16[12,128,40,128]{3,1,0,2:T(8,128)(2,1)} async-done(((bf16[12,128,40,128]{3,1,0,2:T(8,128)(2,1)}), bf16[12,128,40,128]{3,1,0,2:T(8,128)(2,1)}, u32[]{:S(2)}, u32[]{:S(2)}) %all-to-all-start.1) | async-done | bytes 15728672 | tf_op jit(solution)/shard_map/all_to_all | solution.py:66
  581.3 6.9 all-to-all-start.2
  588.1 91.0 %convert_bitcast_fusion = bf16[12,16,40,8,128]{4,3,2,1,0:T(8,128)(2,1)} fusion(bf16[12,128,5120]{2,1,0:T(8,128)(2,1)} %param.9, bf16[5120,5120]{1,0:T(8,128)(2,1)} %param.13), kind=kOutput, calls=%fused_computation.43 | convolution fusion | flops 80538501120 | bytes 83886080 | tf_op jit(solution)/shard_map/bsd,de->bse/dot_general | solution.py:34
  679.1 14.8 %copy.94 = bf16[12,16,40,8,128]{4,3,1,0,2:T(8,128)(2,1)} copy(bf16[12,16,40,8,128]{4,3,2,1,0:T(8,128)(2,1)} %convert_bitcast_fusion) | data formatting | bytes 31457280 | tf_op jit(solution)/shard_map/reshape | solution.py:65
  693.9 65.7 %all-to-all-done.2 = bf16[12,128,40,128]{3,1,0,2:T(8,128)(2,1)} async-done(((bf16[12,128,40,128]{3,1,0,2:T(8,128)(2,1)}), bf16[12,128,40,128]{3,1,0,2:T(8,128)(2,1)}, u32[]{:S(2)}, u32[]{:S(2)}) %all-to-all-start.2) | async-done | bytes 15728672 | tf_op jit(solution)/shard_map/all_to_all | solution.py:67
  759.6 6.8 all-to-all-start
  766.5 0.1 iota_compare_fusion.6
  766.6 0.1 iota_compare_fusion.4
  766.7 0.1 iota_compare_fusion.5
  766.8 0.1 iota_compare_fusion.2
  766.9 0.1 iota_compare_fusion.3
  766.9 0.1 iota_compare_fusion
  767.0 0.1 iota_compare_fusion.1
  767.1 8.1 copy.62
  775.3 0.0 copy-start.1
  775.3 13.0 copy.66
  788.3 3.5 fusion.97
  791.8 4.8 fusion.79
  796.6 8.6 fusion.66
  805.2 7.5 fusion.53
  812.6 12.3 fusion.47
  824.9 14.7 fusion.32
  839.6 13.7 fusion.155
  853.3 16.9 %fusion.26 = f32[12,10,64,448]{3,2,1,0:T(8,128)} fusion(bf16[12,512,10,128]{3,1,2,0:T(8,128)(2,1)} %bitcast.85, bf16[12,512,10,128]{3,1,2,0:T(8,128)(2,1)} %bitcast.98), kind=kOutput, calls=%fused_computation.46 | convolution fusion | flops 880803840 | bytes 29491200 | tf_op jit(solution)/shard_map/bqhd,bkhd->bhqk/dot_general | solution.py:51
  870.2 67.7 %all-to-all-done = bf16[12,128,40,128]{3,1,0,2:T(8,128)(2,1)} async-done(((bf16[12,128,40,128]{3,1,0,2:T(8,128)(2,1)}), bf16[12,128,40,128]{3,1,0,2:T(8,128)(2,1)}, u32[]{:S(2)}, u32[]{:S(2)}) %all-to-all-start) | async-done | bytes 15728672 | tf_op jit(solution)/shard_map/all_to_all | solution.py:68
  937.9 14.9 %copy.58 = bf16[12,4,128,10,128]{4,2,1,3,0:T(8,128)(2,1)} copy(bf16[12,4,128,10,128]{4,2,0,3,1:T(8,128)(2,1)} %bitcast.3) | data formatting | bytes 31457280 | tf_op jit(solution)/shard_map/all_to_all | solution.py:68
  952.8 19.8 %fusion.154 = (f32[12,10,64]{2,1,0:T(8,128)S(1)}, f32[12,10,64,448]{3,2,1,0:T(8,128)}) fusion(f32[12,10,64,448]{3,2,1,0:T(8,128)} %fusion.26, pred[64,448]{1,0:T(8,128)(4,1)S(1)} %iota_compare_fusion.1), kind=kOutput, calls=%fused_computation.194 | output fusion | flops 20644288 | bytes 27584512 | tf_op jit(solution)/shard_map/sub | solution.py:54
  972.6 15.8 %fusion.153 = (f32[12,10,64]{2,1,0:T(8,128)S(1)}, f32[12,10,64,384]{3,2,1,0:T(8,128)}) fusion(f32[12,10,64,384]{3,2,1,0:T(8,128)} %fusion.32, pred[64,384]{1,0:T(8,128)(4,1)S(1)} %iota_compare_fusion.2), kind=kOutput, calls=%fused_computation.193 | output fusion | flops 17695104 | bytes 23648256 | tf_op jit(solution)/shard_map/sub | solution.py:54
  988.4 16.2 %fusion.152 = (f32[12,10,64]{2,1,0:T(8,128)S(1)}, f32[12,10,64,320]{3,2,1,0:T(8,128)}) fusion(f32[12,10,64,320]{3,2,1,0:T(8,128)} %fusion.47, pred[64,320]{1,0:T(8,128)(4,1)S(1)} %iota_compare_fusion.3), kind=kOutput, calls=%fused_computation.192 | output fusion | flops 14745919 | bytes 19712000 | tf_op jit(solution)/shard_map/sub | solution.py:54
  1004.6 11.2 fusion.151
  1015.8 11.5 fusion.150
  1027.3 5.6 fusion.149
  1033.0 0.0 slice-start.3
  1033.0 1.3 fusion.148
  1034.3 0.6 slice-done.3
  1034.9 2.2 bitcast_dynamic-update-slice_fusion.7
  1037.0 3.0 bitcast_dynamic-update-slice_fusion.6
  1040.0 6.2 bitcast_dynamic-update-slice_fusion.5
  1046.2 3.2 bitcast_dynamic-update-slice_fusion.4
  1049.4 6.7 bitcast_dynamic-update-slice_fusion.3
  1056.1 6.7 bitcast_dynamic-update-slice_fusion.2
  1062.8 12.4 bitcast_dynamic-update-slice_fusion.1
  1075.2 13.7 bitcast_dynamic-update-slice_fusion
  1089.0 16.7 %copy.68 = bf16[12,512,10,128]{3,0,2,1:T(8,128)(2,1)} copy(bf16[12,512,10,128]{3,1,2,0:T(8,128)(2,1)} %bitcast_dynamic-update-slice_fusion) | data formatting | bytes 31457280 | tf_op jit(solution)/shard_map/concatenate | solution.py:56
  1105.7 8.1 all-to-all-start.3
  1113.8 227.6 %all-to-all-done.3 = bf16[12,512,10,128]{3,0,2,1:T(8,128)(2,1)} async-done(((bf16[12,512,10,128]{3,0,2,1:T(8,128)(2,1)}), bf16[12,512,10,128]{3,0,2,1:T(8,128)(2,1)}, u32[]{:S(2)}, u32[]{:S(2)}) %all-to-all-start.3) | async-done | bytes 15728672 | tf_op jit(solution)/shard_map/all_to_all | solution.py:70
  1341.4 30.3 %copy.70 = bf16[12,128,4,10,128]{1,4,3,2,0:T(8,128)(2,1)} copy(bf16[12,128,4,10,128]{4,0,3,1,2:T(8,128)(2,1)} %bitcast.25) | data formatting | bytes 31457280 | tf_op jit(solution)/shard_map/all_to_all | solution.py:70
  1371.7 92.8 %fusion.20 = (f32[12,128]{1,0:T(8,128)S(1)}, bf16[12,128,5120]{2,1,0:T(8,128)(2,1)}) fusion(bf16[12,128,5120]{1,2,0:T(8,128)(2,1)} %bitcast.109, bf16[5120,5120]{1,0:T(8,128)(2,1)} %param.14), kind=kOutput, calls=%fused_computation.26 | convolution fusion | flops 80562094080 | bytes 83892224 | tf_op jit(solution)/shard_map/bsd,de->bse/dot_general | solution.py:34
  1464.5 19.0 %fusion.23 = bf16[12,128,5120]{2,1,0:T(8,128)(2,1)} fusion(bf16[12,128,5120]{2,1,0:T(8,128)(2,1)} %get-tuple-element.38, bf16[12,128,5120]{2,1,0:T(8,128)(2,1)} %param.9, f32[5120]{0:T(1024)S(1)} %convert_element_type.148, f32[12,128]{1,0:T(8,128)S(1)} %add_rsqrt_fusion), kind=kLoop, calls=%fused_computation.29 | loop fusion | flops 47185920 | bytes 47212544 | tf_op jit(solution)/shard_map/convert_element_type | solution.py:72
  (42 shorter events, 0.1 us)
Async XLA Ops:
  0.5 91.2 %copy-start.3 = (bf16[5120]{0:T(1024)(128)(2,1)S(1)}, bf16[5120]{0:T(1024)(128)(2,1)}, u32[]{:S(2)}) copy-start(bf16[5120]{0:T(1024)(128)(2,1)} %param.16) | copy-start | bytes 30724
  113.2 91.8 %copy-start.4 = (bf16[5120]{0:T(1024)(128)(2,1)S(1)}, bf16[5120]{0:T(1024)(128)(2,1)}, u32[]{:S(2)}) copy-start(bf16[5120]{0:T(1024)(128)(2,1)} %param.15) | copy-start | bytes 30724
  214.6 11.9 copy-start.6
  226.4 79.7 %copy-start.7 = (f32[64]{0:T(128)S(1)}, f32[64]{0:T(128)}, u32[]{:S(2)}) copy-start(f32[64]{0:T(128)} %negate_power_fusion) | copy-start | bytes 772
  401.6 179.7 %all-to-all-start.1 = ((bf16[12,128,40,128]{3,1,0,2:T(8,128)(2,1)}), bf16[12,128,40,128]{3,1,0,2:T(8,128)(2,1)}, u32[]{:S(2)}, u32[]{:S(2)}) async-start(bf16[12,128,40,128]{3,1,0,2:T(8,128)(2,1)} %pad_maximum_fusion), calls=%async_computation.1 | async-start | bytes 31457280 | tf_op jit(solution)/shard_map/all_to_all | solution.py:66
  581.3 178.3 %all-to-all-start.2 = ((bf16[12,128,40,128]{3,1,0,2:T(8,128)(2,1)}), bf16[12,128,40,128]{3,1,0,2:T(8,128)(2,1)}, u32[]{:S(2)}, u32[]{:S(2)}) async-start(bf16[12,128,40,128]{3,1,0,2:T(8,128)(2,1)} %pad_maximum_fusion.1), calls=%async_computation.2 | async-start | bytes 31457280 | tf_op jit(solution)/shard_map/all_to_all | solution.py:67
  759.6 178.3 %all-to-all-start = ((bf16[12,128,40,128]{3,1,0,2:T(8,128)(2,1)}), bf16[12,128,40,128]{3,1,0,2:T(8,128)(2,1)}, u32[]{:S(2)}, u32[]{:S(2)}) async-start(bf16[12,128,40,128]{3,1,0,2:T(8,128)(2,1)} %bitcast.90), calls=%async_computation | async-start | bytes 31457280 | tf_op jit(solution)/shard_map/all_to_all | solution.py:68
  775.3 16.6 %copy-start.1 = (bf16[12,4,128,10,128]{4,2,1,3,0:T(8,128)(2,1)}, bf16[12,4,128,10,128]{4,2,1,3,0:T(8,128)(2,1)S(1)}, u32[]{:S(2)}) copy-start(bf16[12,4,128,10,128]{4,2,1,3,0:T(8,128)(2,1)S(1)} %copy.62) | copy-start | bytes 47185924
  788.3 16.8 %copy-start = (bf16[12,4,128,10,128]{4,2,1,3,0:T(8,128)(2,1)}, bf16[12,4,128,10,128]{4,2,1,3,0:T(8,128)(2,1)S(1)}, u32[]{:S(2)}) copy-start(bf16[12,4,128,10,128]{4,2,1,3,0:T(8,128)(2,1)S(1)} %copy.66) | copy-start | bytes 47185924
  1015.8 17.2 %copy-start.2 = (f32[12,10,64,64]{2,3,1,0:T(8,128)S(1)}, f32[12,10,64,64]{2,3,1,0:T(8,128)}, u32[]{:S(2)}) copy-start(f32[12,10,64,64]{2,3,1,0:T(8,128)} %fusion.97) | copy-start | bytes 5898244
  1015.8 18.5 %slice-start = ((s8[15728640]{0:T(1024)(128)(4,1)}), s8[4194304]{0:T(1024)(128)(4,1)S(1)}, s32[]{:S(2)}) async-start(s8[15728640]{0:T(1024)(128)(4,1)} %bitcast.101), calls=%async_computation.4 | async-start | bytes 8388608
  1015.8 18.5 %slice-start.1 = ((s8[15728640]{0:T(1024)(128)(4,1)}), s8[4194304]{0:T(1024)(128)(4,1)S(1)}, s32[]{:S(2)}) async-start(s8[15728640]{0:T(1024)(128)(4,1)} %bitcast.101), calls=%async_computation.5 | async-start | bytes 8388608
  1027.3 7.0 slice-start.2
  1033.0 1.9 slice-start.3
  1037.0 9.1 slice-start.4
  1040.0 6.2 slice-start.5
  1062.8 12.4 copy-start.8
  1105.6 8.1 copy-start.5
  1105.7 235.7 %all-to-all-start.3 = ((bf16[12,512,10,128]{3,0,2,1:T(8,128)(2,1)}), bf16[12,512,10,128]{3,0,2,1:T(8,128)(2,1)}, u32[]{:S(2)}, u32[]{:S(2)}) async-start(bf16[12,512,10,128]{3,0,2,1:T(8,128)(2,1)} %copy.68), calls=%async_computation.3 | async-start | bytes 41943040 | tf_op jit(solution)/shard_map/all_to_all | solution.py:70
where the time goes:
time: 1490 us; the launch traced here: 1480 us
  waiting for transfers between devices  514 us (34%)
  matrix products  503 us (34%)
  other arithmetic  236 us (16%)
  local copies, waits for them, and re-layouts  202 us (14%)
  starting transfers between devices  29 us (2%)
    dot_general x4, matrix products, project(): jnp.einsum('bsd,de->bse', x_tok, weight, preferred_element_type=jnp.float32)  367 us
    all_to_all x1, waiting for transfers between devices, local_block(): lax.all_to_all(o_heads, 'sp', 1, 2, tiled=True)  228 us
    all_to_all x1, waiting for transfers between devices, local_block(): q_heads = lax.all_to_all(q_loc, 'sp', 2, 1, tiled=True)  153 us
    sub x7, other arithmetic, causal_attention(): probs = jax.nn.softmax(scores, axis=-1).astype(jnp.bfloat16)  81.4 us
    slice x1, local copies, waits for them, and re-layouts, apply_rope(): first = heads_f32[..., :half]  79.7 us
    another operation x1, other arithmetic  72.7 us
    dot_general x7, matrix products, causal_attention(): jnp.einsum('bqhd,bkhd->bhqk', q_blk, k_heads[:, :key_end], preferred_elem...  68.2 us
    all_to_all x1, waiting for transfers between devices, local_block(): v_heads = lax.all_to_all(v_loc, 'sp', 2, 1, tiled=True)  67.7 us
  transfers between devices with their start and end apart: 4, of which 4 were waited for; matrix products, arithmetic and copies ran while one was open for 15% of the time, Pallas kernels for 0%

commit v1 on v0

v1 whole, which is shorter than its diff:
```python
import functools

import jax
import jax.numpy as jnp
from jax import lax
from jax.experimental import pallas as pl
from jax.experimental.pallas import tpu as pltpu
from jax.sharding import PartitionSpec as P


HEAD_DIM = 128
ROPE_THETA = 500000.0
NORM_EPS = 1e-6
SCALE = HEAD_DIM ** -0.5
LOG2E = 1.4426950408889634
QKV_TILE = 1024
OUT_TILE = 512
HEADS_PER_STEP = 4
VMEM_BYTES = 63 * 2 ** 20


def rope_tables(pos_ids):
    inv_freq = 1.0 / (ROPE_THETA ** (jnp.arange(0, HEAD_DIM, 2, dtype=jnp.float32) / HEAD_DIM))
    angles = pos_ids.astype(jnp.float32)[..., None] * inv_freq
    cos_t, sin_t = jnp.cos(angles), jnp.sin(angles)
    return jnp.concatenate([cos_t, cos_t], axis=-1), jnp.concatenate([-sin_t, sin_t], axis=-1)


def lane_sums(sq):
    part = sq[:, :128]
    for col in range(1, sq.shape[1] // 128):
        part = part + sq[:, col * 128:(col + 1) * 128]
    return part


def row_copies(srcs, dst, sems):
    return [pltpu.make_async_copy(src, dst.at[pl.ds(i * 128, 128), :], sems.at[i]) for i, src in enumerate(srcs)]


def qkv_kernel(n_tiles, own, counts, aliased, *refs):
    n_pieces = len(counts)
    x_hbm = refs[:n_pieces]
    weights = refs[n_pieces:n_pieces + 3]
    qkv_out, stat_out, x_buf, w_buf, x_sem, w_sem = refs[n_pieces + 4 + 2 * aliased:]
    step = pl.program_id(0)
    slot = lax.rem(step, 2)

    def fetch(at_step):
        for idx, w_ref in enumerate(weights):
            @pl.when(at_step // n_tiles == idx)
            def _():
                cols = pl.ds(pl.multiple_of(lax.rem(at_step, n_tiles) * QKV_TILE, QKV_TILE), QKV_TILE)
                to = lax.rem(at_step, 2)
                pltpu.make_async_copy(w_ref.at[:, cols], w_buf.at[to], w_sem.at[to]).start()

    @pl.when(step == 0)
    def _():
        srcs = []
        for idx, (ref, count) in enumerate(zip(x_hbm, counts)):
            base = lax.axis_index('sp') * count if own and idx == 0 else 0
            srcs += [ref.at[base + b] for b in range(count)]
        copies = row_copies(srcs, x_buf, x_sem)
        for cp in copies:
            cp.start()
        fetch(step)
        for cp in copies:
            cp.wait()

    @pl.when(step + 1 < 3 * n_tiles)
    def _():
        fetch(step + 1)

    pltpu.make_async_copy(weights[0].at[:, pl.ds(0, QKV_TILE)], w_buf.at[slot], w_sem.at[slot]).wait()
    proj = jnp.dot(x_buf[...], w_buf[slot], preferred_element_type=jnp.float32).astype(jnp.bfloat16)
    qkv_out[...] = proj.reshape(qkv_out.shape)
    wide = proj.astype(jnp.float32)
    part = lane_sums(wide * wide).reshape(stat_out.shape)
    first = lax.rem(step, n_tiles) == 0

    @pl.when(first)
    def _():
        stat_out[...] = part

    @pl.when(jnp.logical_not(first))
    def _():
        stat_out[...] = stat_out[...] + part


def qkv_call(pieces, counts, own, weights, per_dev, group, batch_block, prior, after):
    width = weights[0].shape[0]
    n_tiles = width // QKV_TILE
    n_batch = sum(counts) // 2
    rows = sum(counts) * 128
    any_spec = pl.BlockSpec(memory_space=pl.ANY)
    n_in = len(pieces) + 4
    return pl.pallas_call(
        functools.partial(qkv_kernel, n_tiles, own, counts, bool(prior)),
        grid=(3 * n_tiles,),
        in_specs=[any_spec] * (n_in + len(prior)),
        out_specs=[
            pl.BlockSpec((1, 2, n_batch, 128, QKV_TILE), lambda s: (s // n_tiles, group, batch_block, 0, lax.rem(s, n_tiles))),
            pl.BlockSpec((1, 2, n_batch, 128, 128), lambda s: (s // n_tiles, group, batch_block, 0, 0))],
        out_shape=[jax.ShapeDtypeStruct((3, 4, per_dev, 128, width), jnp.bfloat16),
                   jax.ShapeDtypeStruct((3, 4, per_dev, 128, 128), jnp.float32)],
        input_output_aliases={n_in: 0, n_in + 1: 1} if prior else {},
        scratch_shapes=[pltpu.VMEM((rows, width), jnp.bfloat16), pltpu.VMEM((2, width, QKV_TILE), jnp.bfloat16),
                        pltpu.SemaphoreType.DMA((sum(counts),)), pltpu.SemaphoreType.DMA((2,))],
        compiler_params=pltpu.CompilerParams(vmem_limit_bytes=VMEM_BYTES, dimension_semantics=("arbitrary",)),
        cost_estimate=pl.CostEstimate(flops=6 * rows * width * width, transcendentals=0, bytes_accessed=6 * width * width),
    )(*pieces, *weights, after, *prior)


def attention_kernel(width, dev_ref, *refs):
    qkv_refs, stat_refs = refs[:4], refs[4:8]
    cos_ref, sin_ref, gq_ref, gk_ref, out_ref, cos_n, sin_n = refs[8:]
    dev = dev_ref[0]

    @pl.when(pl.program_id(1) == 0)
    def _():
        for which in range(2):
            for j in range(4):
                rows = slice(j * 128, (j + 1) * 128)
                total = jnp.sum(stat_refs[j][which, 0, 0], axis=-1, keepdims=True)
                inv = lax.rsqrt(total * (1.0 / width) + NORM_EPS)
                cos_n[which, rows, :] = cos_ref[0, rows, :] * inv
                sin_n[which, rows, :] = sin_ref[0, rows, :] * inv

    row_id = lax.broadcasted_iota(jnp.int32, (128, 128), 0)
    col_id = lax.broadcasted_iota(jnp.int32, (128, 128), 1)
    causal = col_id <= row_id
    factor = SCALE * LOG2E
    zeros = jnp.zeros((128, 128), jnp.bfloat16)

    def scores(q, k):
        return lax.dot_general(q, k, (((1,), (1,)), ((), ())), preferred_element_type=jnp.float32)

    def prepare(h):
        lanes = slice(h * 128, (h + 1) * 128)
        parts = ([], [])
        for which, gain_ref in ((0, gq_ref), (1, gk_ref)):
            gain = gain_ref[:, lanes].astype(jnp.float32)
            for j in range(4):
                rows = slice(j * 128, (j + 1) * 128)
                u = qkv_refs[j][which, 0, 0, :, lanes].astype(jnp.float32) * gain
                rot = u * cos_n[which, rows, :] + pltpu.roll(u, 64, 1) * sin_n[which, rows, :]
                parts[which].append(rot.astype(jnp.bfloat16))
        q, k = parts
        k_lo, k_hi = jnp.concatenate(k[:2], axis=0), jnp.concatenate(k[2:], axis=0)
        return scores(jnp.concatenate(q, axis=0), k_lo), scores(jnp.concatenate(q[2:], axis=0), k_hi)

    def finish(h, s_lo, s_hi):
        lanes = slice(h * 128, (h + 1) * 128)
        probs = []
        for j in range(4):
            blocks = []
            for c in range(j + 1):
                src, r = (s_lo, j) if c < 2 else (s_hi, j - 2)
                blk = src[r * 128:(r + 1) * 128, (c % 2) * 128:(c % 2 + 1) * 128]
                blocks.append(jnp.where(causal, blk, -1e30) if c == j else blk)
            top = functools.reduce(jnp.maximum, blocks)
            top = jnp.max(top, axis=-1, keepdims=True) * factor
            exps = [jnp.exp2(blk * factor - top) for blk in blocks]
            inv = 1.0 / jnp.sum(functools.reduce(jnp.add, exps), axis=-1, keepdims=True)
            row = [(e * inv).astype(jnp.bfloat16) for e in exps]
            probs.append(row + [zeros] * (4 - len(row)))
        p_lo = jnp.concatenate([jnp.concatenate(p[:2], axis=1) for p in probs], axis=0)
        p_hi = jnp.concatenate([jnp.concatenate(p[2:], axis=1) for p in probs[2:]], axis=0)
        v = [qkv_refs[j][2, 0, 0, :, lanes] for j in range(4)]
        o_lo = jnp.dot(p_lo, jnp.concatenate(v[:2], axis=0), preferred_element_type=jnp.float32)
        o_hi = jnp.dot(p_hi, jnp.concatenate(v[2:], axis=0), preferred_element_type=jnp.float32)
        for j in range(4):
            o = o_lo[j * 128:(j + 1) * 128]
            if j >= 2:
                o = o + o_hi[(j - 2) * 128:(j - 1) * 128]
            out_ref[jnp.bitwise_xor(dev, j), 0, :, lanes] = o.astype(jnp.bfloat16)

    ready = prepare(0)
    for h in range(HEADS_PER_STEP):
        following = prepare(h + 1) if h + 1 < HEADS_PER_STEP else None
        finish(h, *ready)
        ready = following


def attention_call(qkv, stats, dev, first, n_batch, cos_t, sin_t, gain_q, gain_k):
    width = qkv.shape[-1]
    cols = HEADS_PER_STEP * 128

    def qkv_map(j):
        return lambda b, h, dev_ref: (0, jnp.bitwise_xor(dev_ref[0], j), b + first, 0, h)

    def stat_map(j):
        return lambda b, h, dev_ref: (0, jnp.bitwise_xor(dev_ref[0], j), b + first, 0, 0)

    table_spec = pl.BlockSpec((1, 512, 128), lambda b, h, dev_ref: (b + first, 0, 0))
    gain_spec = pl.BlockSpec((1, cols), lambda b, h, dev_ref: (0, h))
    n_heads = width // 128
    return pl.pallas_call(
        functools.partial(attention_kernel, width),
        grid_spec=pltpu.PrefetchScalarGridSpec(
            num_scalar_prefetch=1,
            grid=(n_batch, width // cols),
            in_specs=[pl.BlockSpec((3, 1, 1, 128, cols), qkv_map(j)) for j in range(4)]
            + [pl.BlockSpec((2, 1, 1, 128, 128), stat_map(j)) for j in range(4)] + [table_spec] * 2 + [gain_spec] * 2,
            out_specs=pl.BlockSpec((4, 1, 128, cols), lambda b, h, dev_ref: (0, b, 0, h)),
            scratch_shapes=[pltpu.VMEM((2, 512, 128), jnp.float32)] * 2,
        ),
        out_shape=jax.ShapeDtypeStruct((4, n_batch, 128, width), jnp.bfloat16),
        compiler_params=pltpu.CompilerParams(vmem_limit_bytes=VMEM_BYTES, dimension_semantics=("arbitrary", "arbitrary")),
        cost_estimate=pl.CostEstimate(flops=n_batch * n_heads * 512 * 512 * 128 * 8, transcendentals=0,
                                      bytes_accessed=n_batch * 512 * width * 8),
    )(dev, *[qkv] * 4, *[stats] * 4, cos_t, sin_t, gain_q.reshape(1, width), gain_k.reshape(1, width))


def out_kernel(n_tiles, rel, o_counts, x_counts, own, moved, *refs):
    n_o, n_x, n_z = len(o_counts), len(x_counts), len(moved)
    pos = 0

    def take(n):
        nonlocal pos
        pos += n
        return refs[pos - n:pos]

    o_hbm, x_hbm, z_hbm = take(n_o), take(n_x), take(n_z)
    w_hbm, gain_ref, _ = take(3)
    y_hbm = take(n_x)
    o_buf, x_buf, a_buf, ss_buf, w_buf, o_sem, x_sem, y_sem, w_sem = take(9)
    z_buf, z_sem = take(2) if n_z else (None, None)
    step = pl.program_id(0)
    width = o_buf.shape[1]
    slot = lax.rem(step, 2)
    dev = lax.axis_index('sp')

    def fetch(at_step):
        cols = pl.ds(pl.multiple_of(at_step * OUT_TILE, OUT_TILE), OUT_TILE)
        to = lax.rem(at_step, 2)
        return pltpu.make_async_copy(w_hbm.at[:, cols], w_buf.at[to], w_sem.at[to])

    def at_pieces(piece_refs):
        out = []
        for idx, (ref, count) in enumerate(zip(piece_refs, x_counts)):
            base = dev * count if own and idx == 0 else 0
            out += [ref.at[base + b] for b in range(count)]
        return out

    def z_copies(outward):
        copies, i = [], 0
        for ref, (r, count, per_dev) in zip(z_hbm, moved):
            base = jnp.bitwise_xor(dev, r) * per_dev
            for b in range(count):
                src, dst = (z_buf.at[i], y_hbm[0].at[base + b]) if outward else (ref.at[b], z_buf.at[i])
                copies.append(pltpu.make_async_copy(src, dst, z_sem.at[int(outward), i]))
                i += 1
        return copies

    @pl.when(step == 0)
    def _():
        fetch(step).start()
        srcs = [ref.at[r, b] for r in rel for ref, count in zip(o_hbm, o_counts) for b in range(count)]
        copies = row_copies(srcs, o_buf, o_sem)
        for cp in copies:
            cp.start()
        for cp in copies:
            cp.wait()
        for cp in row_copies(at_pieces(x_hbm), x_buf, x_sem):
            cp.start()

    @pl.when(step + 1 < n_tiles)
    def _():
        fetch(step + 1).start()

    if n_z:
        @pl.when(step == 1)
        def _():
            for cp in z_copies(False):
                cp.start()

        @pl.when(step == 3)
        def _():
            for cp in z_copies(False):
                cp.wait()
            for cp in z_copies(True):
                cp.start()

    fetch(step).wait()
    a_tile = jnp.dot(o_buf[...], w_buf[slot], preferred_element_type=jnp.float32).astype(jnp.bfloat16)
    a_buf[step] = a_tile
    wide = a_tile.astype(jnp.float32)
    part = lane_sums(wide * wide)

    @pl.when(step == 0)
    def _():
        ss_buf[...] = part

    @pl.when(step != 0)
    def _():
        ss_buf[...] = ss_buf[...] + part

    @pl.when(step == n_tiles - 1)
    def _():
        for cp in row_copies(at_pieces(x_hbm), x_buf, x_sem):
            cp.wait()
        copies = []
        for i, dst in enumerate(at_pieces(y_hbm)):
            rows = slice(i * 128, (i + 1) * 128)
            inv = lax.rsqrt(jnp.sum(ss_buf[rows, :], axis=-1, keepdims=True) * (1.0 / width) + NORM_EPS)
            for t in range(n_tiles):
                cols = slice(t * OUT_TILE, (t + 1) * OUT_TILE)
                normed = a_buf[t, rows, :].astype(jnp.float32) * inv * gain_ref[:, cols].astype(jnp.float32)
                x_buf[rows, cols] = (x_buf[rows, cols].astype(jnp.float32) + normed).astype(jnp.bfloat16)
            cp = pltpu.make_async_copy(x_buf.at[pl.ds(i * 128, 128), :], dst, y_sem.at[i])
            cp.start()
            copies.append(cp)
        for cp in copies:
            cp.wait()
        if n_z:
            for cp in z_copies(True):
                cp.wait()


def out_call(o_list, rel, x_list, x_counts, own, out_batches, w_out, gain_out, after, z_list=(), moved=()):
    width = w_out.shape[0]
    n_tiles = width // OUT_TILE
    o_counts = tuple(o.shape[1] for o in o_list)
    rows = sum(x_counts) * 128
    any_spec = pl.BlockSpec(memory_space=pl.ANY)
    n_moved = sum(m[1] for m in moved)
    extra = [pltpu.VMEM((n_moved, 128, width), jnp.bfloat16), pltpu.SemaphoreType.DMA((2, n_moved))] if moved else []
    return pl.pallas_call(
        functools.partial(out_kernel, n_tiles, rel, o_counts, x_counts, own, moved),
        grid=(n_tiles,),
        in_specs=[any_spec] * (len(o_list) + len(x_list) + len(z_list) + 1)
        + [pl.BlockSpec((1, width), lambda step: (0, 0)), any_spec],
        out_specs=[any_spec] * len(x_list),
        out_shape=[jax.ShapeDtypeStruct((n, 128, width), jnp.bfloat16) for n in out_batches],
        scratch_shapes=[pltpu.VMEM((rows, width), jnp.bfloat16), pltpu.VMEM((rows, width), jnp.bfloat16),
                        pltpu.VMEM((n_tiles, rows, OUT_TILE), jnp.bfloat16), pltpu.VMEM((rows, 128), jnp.float32),
                        pltpu.VMEM((2, width, OUT_TILE), jnp.bfloat16)]
        + [pltpu.SemaphoreType.DMA((rows // 128,))] * 3 + [pltpu.SemaphoreType.DMA((2,))] + extra,
        compiler_params=pltpu.CompilerParams(vmem_limit_bytes=VMEM_BYTES, dimension_semantics=("arbitrary",)),
        cost_estimate=pl.CostEstimate(flops=2 * rows * width * width, transcendentals=0, bytes_accessed=2 * width * width),
    )(*o_list, *x_list, *z_list, w_out, gain_out.reshape(1, width), after)


def solution(mesh):
    def local_block(x_loc, pos_loc, w_query, w_key, w_value, w_out, gain_q, gain_k, gain_out):
        batch, _, _ = x_loc.shape
        per_dev = batch // 4
        dev = lax.axis_index('sp')

        def swap(arr, r):
            return lax.ppermute(arr, 'sp', [(i, i ^ r) for i in range(4)])

        def piece(r, first, count):
            return lax.dynamic_slice_in_dim(x_loc, (dev ^ r) * per_dev + first, count, axis=0)

        x_far01 = [swap(piece(r, 0, 2), r) for r in (2, 3)]
        x_near = swap(piece(1, 0, per_dev), 1)
        pos_parts = [lax.dynamic_slice_in_dim(pos_loc, dev * per_dev, per_dev, axis=0)]
        for r in range(1, 4):
            pos_parts.append(swap(lax.dynamic_slice_in_dim(pos_loc, (dev ^ r) * per_dev, per_dev, axis=0), r))

        weights = (w_query, w_key, w_value)
        dev_arr = jnp.full((1,), dev, jnp.int32)
        near = qkv_call([x_loc, x_near], (per_dev, per_dev), True, weights, per_dev, 0, 0, (), gain_q)
        p2, p3, x_far01[0], x_far01[1] = lax.optimization_barrier((piece(2, 2, 1), piece(3, 2, 1), x_far01[0], x_far01[1]))
        x_far2 = [swap(p2, 2), swap(p3, 3)]
        qkv01, stats01 = qkv_call(x_far01, (2, 2), False, weights, per_dev, 1, 0, near, gain_q)
        pos_parts, _ = lax.optimization_barrier((pos_parts, near[1]))
        pos_rel = jnp.stack(pos_parts)
        pos_mine = jnp.concatenate([lax.dynamic_index_in_dim(pos_rel, dev ^ j, axis=0, keepdims=False) for j in range(4)], axis=1)
        cos_t, sin_t = rope_tables(pos_mine)
        o01 = attention_call(qkv01, stats01, dev_arr, 0, 2, cos_t, sin_t, gain_q, gain_k)
        y_far01 = out_call([o01], (2, 3), x_far01, (2, 2), False, (2, 2), w_out, gain_out, gain_q)
        z_far01 = [swap(y_far01[0], 2), swap(y_far01[1], 3)]
        qkv2, stats2 = qkv_call(x_far2, (1, 1), False, weights, per_dev, 1, 2, (qkv01, stats01), y_far01[0])
        o2 = attention_call(qkv2, stats2, dev_arr, 2, 1, cos_t, sin_t, gain_q, gain_k)
        y_far2 = out_call([o2], (2, 3), x_far2, (1, 1), False, (1, 1), w_out, gain_out, gain_q)
        z_far2 = [swap(y_far2[0], 2), swap(y_far2[1], 3)]
        y_all, y_near = out_call([o01, o2], (0, 1), [x_loc, x_near], (per_dev, per_dev), True, (batch, per_dev), w_out, gain_out,
                                 y_far2[0], z_far01, ((2, 2, per_dev), (3, 2, per_dev)))
        z_near = swap(y_near, 1)

        def put(acc, part, r, first):
            return lax.dynamic_update_slice_in_dim(acc, part, (dev ^ r) * per_dev + first, axis=0)

        y_all = put(y_all, z_near, 1, 0)
        y_all = put(y_all, z_far2[0], 2, 2)
        y_all = put(y_all, z_far2[1], 3, 2)
        return y_all

    tok_spec = P('dp', 'sp', None)

    return jax.shard_map(local_block, mesh=mesh, in_specs=(tok_spec, P('dp', 'sp'), P(), P(), P(), P(), P(), P(), P()), out_specs=tok_spec, check_vma=False)
```

time: 1490 us -> 692 us (0.46)
  matrix products: 503 us -> 0 us
  Pallas kernels: 0 us -> 497 us
  waiting for transfers between devices: 514 us -> 159 us
  other arithmetic: 236 us -> 4.53 us
  local copies, waits for them, and re-layouts: 202 us -> 18.6 us
  starting transfers between devices: 29 us -> 12.2 us
    all_to_all x4 -> x0, waiting for transfers between devices: 514 us -> none  [the longest x1 228 us: local_block(): lax.all_to_all(o_heads, 'sp', 1, 2, tiled=True)]
    pallas_call x0 -> x8, Pallas kernels: none -> 497 us  [the longest x3 285 us: qkv_call(): pl.pallas_call(functools.partial(qkv_kernel, n_tiles, own, counts, bool(p...]
    dot_general x19 -> x0, matrix products: 489 us -> none  [the longest x4 367 us: project(): jnp.einsum('bsd,de->bse', x_tok, weight, preferred_element_type=jnp.float32)]
    ppermute x0 -> x13, waiting for transfers between devices: none -> 159 us  [swap(): return lax.ppermute(arr, 'sp', [(i, i ^ r) for i in range(4)])]
    sub x7 -> x0, other arithmetic: 81.4 us -> none  [causal_attention(): probs = jax.nn.softmax(scores, axis=-1).astype(jnp.bfloat16)]
    slice x1 -> x0, local copies, waits for them, and re-layouts: 79.7 us -> none  [apply_rope(): first = heads_f32[..., :half]]
    another operation x1, other arithmetic: 72.7 us -> 0.01 us  [local_block(): pos_rel = jnp.stack(pos_parts)]
    all_to_all x4 -> x0, local copies, waits for them, and re-layouts: 66.4 us -> none  [the longest x1 30.3 us: local_block(): lax.all_to_all(o_heads, 'sp', 1, 2, tiled=True)]
  transfers between devices with their start and end apart: 4 -> 13, of which waited for: 4 -> 5; matrix products, arithmetic and copies ran while one was open for 15% -> 3% of each run, Pallas kernels for 0% -> 64%
where the time goes in v1:
time: 692 us; the launch traced here: 691 us
  Pallas kernels  497 us (72%)
  waiting for transfers between devices  159 us (23%)
  local copies, waits for them, and re-layouts  18.6 us (3%)
  starting transfers between devices  12.2 us (2%)
    pallas_call x3, Pallas kernels, qkv_call(): pl.pallas_call(functools.partial(qkv_kernel, n_tiles, own, counts, bool(p...  285 us
    ppermute x13, waiting for transfers between devices, swap(): return lax.ppermute(arr, 'sp', [(i, i ^ r) for i in range(4)])  159 us
    pallas_call x3, Pallas kernels, out_call(): pl.pallas_call(functools.partial(out_kernel, n_tiles, rel, o_counts, x_co...  122 us
    pallas_call x2, Pallas kernels, attention_call(): pl.pallas_call(functools.partial(attention_kernel, width), grid_spec=pltp...  89.6 us
  transfers between devices with their start and end apart: 13, of which 5 were waited for; matrix products, arithmetic and copies ran while one was open for 3% of the time, Pallas kernels for 64%

profile of v1, /device:TPU:0, one launch (start us, length us, event | category | flops | bytes accessed | tf_op | source)
XLA Modules:
  0.0 691.3 jit_solution(17410038479260368180)
XLA Ops:
  0.0 4.3 constant_dynamic-slice_fusion.8
  4.3 0.7 collective-permute-start.2
  5.0 0.0 copy-start.3
  5.0 0.0 copy-start.1
  5.0 0.0 copy-start.2
  5.0 0.0 copy-start
  5.0 4.6 constant_dynamic-slice_fusion.9
  9.6 2.6 collective-permute-start.1
  12.2 0.0 collective-permute-start
  12.2 0.0 copy-done.3
  12.2 1.4 collective-permute-start.5
  13.6 0.8 collective-permute-start.3
  14.4 0.0 copy-done.1
  14.4 0.6 reshape.54.refs_4_.refs_7_
  15.0 0.0 copy-done.2
  15.0 0.6 reshape.53.refs_11_
  15.6 0.0 copy-done
  15.6 0.6 reshape.52.refs_10_
  16.3 3.4 constant_dynamic-slice_fusion.11
  19.6 50.2 %collective-permute-done.1.refs_1_.refs_2_ = bf16[2,128,5120]{2,1,0:T(8,128)(2,1)} collective-permute-done((bf16[2,128,5120]{2,1,0:T(8,128)(2,1)}, bf16[2,128,5120]{2,1,0:T(8,128)(2,1)}, u32[]{:S(2)}, u32[]{:S(2)}) %collective-permute-start.1) | collective-permute-done | bytes 2621472 | tf_op jit(solution)/shard_map/ppermute | solution.py:351
  69.8 1.1 collective-permute-start.4
  70.9 55.3 %collective-permute-done.refs_0_.refs_1_ = bf16[2,128,5120]{2,1,0:T(8,128)(2,1)} collective-permute-done((bf16[2,128,5120]{2,1,0:T(8,128)(2,1)S(1)}, bf16[2,128,5120]{2,1,0:T(8,128)(2,1)}, u32[]{:S(2)}, u32[]{:S(2)}) %collective-permute-start) | collective-permute-done | bytes 2621472 | tf_op jit(solution)/shard_map/ppermute | solution.py:351
  126.2 1.6 collective-permute-start.6
  127.8 0.0 collective-permute-done.2.refs_1_.refs_3_
  127.8 0.0 collective-permute-start.7
  127.8 133.5 %shard_map.91 = (bf16[3,4,3,128,5120]{4,3,2,1,0:T(8,128)(2,1)}, f32[3,4,3,128,128]{4,3,2,1,0:T(8,128)}) custom-call(bf16[12,128,5120]{2,1,0:T(8,128)(2,1)} %refs_2_.7, bf16[3,128,5120]{2,1,0:T(8,128)(2,1)} %collective-permute-done.2.refs_1_.refs_3_, bf16[5120,5120]{1,0:T(8,128)(2,1)} %refs_2_.6, bf16[5120,5120]{1,0:T(8,128)(2,1)} %refs_3_.8, ...), custom_call_target="tpu_custom_call" | custom-call | flops 120795955200 | bytes 157286400 | tf_op jit(solution)/shard_map/pallas_call | solution.py:96
  261.3 0.0 collective-permute-done.5
  261.3 0.0 collective-permute-done.3
  261.3 0.0 collective-permute-done.4
  261.4 2.8 fusion
  264.2 1.7 pad_maximum_fusion
  265.9 91.6 %shard_map.92 = (bf16[3,4,3,128,5120]{4,3,2,1,0:T(8,128)(2,1)}, f32[3,4,3,128,128]{4,3,2,1,0:T(8,128)}) custom-call(bf16[2,128,5120]{2,1,0:T(8,128)(2,1)} %collective-permute-done.refs_0_.refs_1_, bf16[2,128,5120]{2,1,0:T(8,128)(2,1)} %collective-permute-done.1.refs_1_.refs_2_, ...), custom_call_target="tpu_custom_call", output_to_operand_aliasing={{0}: (6, {}), {1}: (7, {})} | custom-call | flops 80530636800 | bytes 157286400 | tf_op jit(solution)/shard_map/pallas_call | solution.py:96
  357.5 59.2 %shard_map.93.refs_0_ = bf16[4,2,128,5120]{3,2,1,0:T(8,128)(2,1)} custom-call(s32[1]{0:T(128)} %bitcast.dev_ref, bf16[3,4,3,128,5120]{4,3,2,1,0:T(8,128)(2,1)} %get-tuple-element.29.refs_0_.refs_1_.refs_2_.refs_3_.refs_6_, bf16[3,4,3,128,5120]{4,3,2,1,0:T(8,128)(2,1)} %get-tuple-element.29.refs_0_.refs_1_.refs_2_.refs_3_.refs_6_, ...), custom_call_target="tpu_custom_call" | custom-call | flops 21474836480 | bytes 41943040 | tf_op jit(solution)/shard_map/pallas_call | solution.py:197
  416.7 39.1 %shard_map.94 = (bf16[2,128,5120]{2,1,0:T(8,128)(2,1)}, bf16[2,128,5120]{2,1,0:T(8,128)(2,1)}) custom-call(bf16[4,2,128,5120]{3,2,1,0:T(8,128)(2,1)} %shard_map.93.refs_0_, bf16[2,128,5120]{2,1,0:T(8,128)(2,1)} %collective-permute-done.refs_0_.refs_1_, bf16[2,128,5120]{2,1,0:T(8,128)(2,1)} %collective-permute-done.1.refs_1_.refs_2_, ...), custom_call_target="tpu_custom_call" | custom-call | flops 26843545600 | bytes 52428800 | tf_op jit(solution)/shard_map/pallas_call | solution.py:328
  455.9 1.7 collective-permute-start.9
  457.6 0.3 collective-permute-start.8
  457.9 0.0 collective-permute-done.6.refs_0_.refs_1_
  457.9 0.0 collective-permute-done.7.refs_1_.refs_2_
  457.9 59.9 %shard_map.95 = (bf16[3,4,3,128,5120]{4,3,2,1,0:T(8,128)(2,1)}, f32[3,4,3,128,128]{4,3,2,1,0:T(8,128)}) custom-call(bf16[1,128,5120]{2,1,0:T(8,128)(2,1)} %collective-permute-done.6.refs_0_.refs_1_, bf16[1,128,5120]{2,1,0:T(8,128)(2,1)} %collective-permute-done.7.refs_1_.refs_2_, ...), custom_call_target="tpu_custom_call", output_to_operand_aliasing={{0}: (6, {}), {1}: (7, {})} | custom-call | flops 40265318400 | bytes 157286400 | tf_op jit(solution)/shard_map/pallas_call | solution.py:96
  517.9 30.4 %shard_map.96.refs_0_.refs_1_ = bf16[4,1,128,5120]{3,2,1,0:T(8,128)(2,1)} custom-call(s32[1]{0:T(128)} %bitcast.dev_ref, bf16[3,4,3,128,5120]{4,3,2,1,0:T(8,128)(2,1)} %get-tuple-element.38.refs_0_.refs_1_.refs_2_.refs_3_, bf16[3,4,3,128,5120]{4,3,2,1,0:T(8,128)(2,1)} %get-tuple-element.38.refs_0_.refs_1_.refs_2_.refs_3_, ...), custom_call_target="tpu_custom_call" | custom-call | flops 10737418240 | bytes 20971520 | tf_op jit(solution)/shard_map/pallas_call | solution.py:197
  548.2 28.0 %shard_map.97 = (bf16[1,128,5120]{2,1,0:T(8,128)(2,1)}, bf16[1,128,5120]{2,1,0:T(8,128)(2,1)}) custom-call(bf16[4,1,128,5120]{3,2,1,0:T(8,128)(2,1)} %shard_map.96.refs_0_.refs_1_, bf16[1,128,5120]{2,1,0:T(8,128)(2,1)} %collective-permute-done.6.refs_0_.refs_1_, bf16[1,128,5120]{2,1,0:T(8,128)(2,1)} %collective-permute-done.7.refs_1_.refs_2_, ...), custom_call_target="tpu_custom_call" | custom-call | flops 13421772800 | bytes 52428800 | tf_op jit(solution)/shard_map/pallas_call | solution.py:328
  576.2 0.0 collective-permute-done.9.refs_5_
  576.3 0.0 collective-permute-done.8.refs_4_
  576.3 54.9 %shard_map.98 = (bf16[12,128,5120]{2,1,0:T(8,128)(2,1)}, bf16[3,128,5120]{2,1,0:T(8,128)(2,1)}) custom-call(bf16[4,2,128,5120]{3,2,1,0:T(8,128)(2,1)} %shard_map.93.refs_0_, bf16[4,1,128,5120]{3,2,1,0:T(8,128)(2,1)} %shard_map.96.refs_0_.refs_1_, bf16[12,128,5120]{2,1,0:T(8,128)(2,1)} %refs_2_.7, ...), custom_call_target="tpu_custom_call" | custom-call | flops 40265318400 | bytes 52428800 | tf_op jit(solution)/shard_map/pallas_call | solution.py:328
  631.1 0.0 collective-permute-start.10
  631.2 1.7 collective-permute-start.11
  632.9 0.1 collective-permute-start.12
  633.0 5.1 collective-permute-done.10
  638.2 2.2 constant_dynamic-update-slice_fusion.2
  640.3 22.7 %collective-permute-done.11 = bf16[1,128,5120]{2,1,0:T(8,128)(2,1)S(1)} collective-permute-done((bf16[1,128,5120]{2,1,0:T(8,128)(2,1)}, bf16[1,128,5120]{2,1,0:T(8,128)(2,1)S(1)}, u32[]{:S(2)}, u32[]{:S(2)}) %collective-permute-start.11) | collective-permute-done | bytes 1310752 | tf_op jit(solution)/shard_map/ppermute | solution.py:351
  663.1 1.1 constant_dynamic-update-slice_fusion.1
  664.2 25.9 %collective-permute-done.12 = bf16[1,128,5120]{2,1,0:T(8,128)(2,1)S(1)} collective-permute-done((bf16[1,128,5120]{2,1,0:T(8,128)(2,1)}, bf16[1,128,5120]{2,1,0:T(8,128)(2,1)S(1)}, u32[]{:S(2)}, u32[]{:S(2)}) %collective-permute-start.12) | collective-permute-done | bytes 1310752 | tf_op jit(solution)/shard_map/ppermute | solution.py:351
  690.2 1.1 constant_dynamic-update-slice_fusion
  (5 shorter events, 0.1 us)
Async XLA Ops:
  4.3 123.5 %collective-permute-start.2 = (bf16[3,128,5120]{2,1,0:T(8,128)(2,1)}, bf16[3,128,5120]{2,1,0:T(8,128)(2,1)}, u32[]{:S(2)}, u32[]{:S(2)}) collective-permute-start(bf16[3,128,5120]{2,1,0:T(8,128)(2,1)} %constant_dynamic-slice_fusion.8), channel_id=1, source_target_pairs={{0,1},{1,0},{2,3},{3,2},{4,5},{5,4},{6,7},{7,6},{8,9},{9,8},{10,11... | collective-permute-start | bytes 11796488 | tf_op jit(solution)/shard_map/ppermute | solution.py:351
  5.0 7.2 %copy-start.3 = (s32[12,128]{1,0:T(8,128)S(1)}, s32[12,128]{1,0:T(8,128)}, u32[]{:S(2)}) copy-start(s32[12,128]{1,0:T(8,128)} %param.10) | copy-start | bytes 18436
  5.0 9.4 %copy-start.1 = (bf16[5120]{0:T(1024)(128)(2,1)S(1)}, bf16[5120]{0:T(1024)(128)(2,1)}, u32[]{:S(2)}) copy-start(bf16[5120]{0:T(1024)(128)(2,1)} %param.17) | copy-start | bytes 30724
  5.0 10.0 %copy-start.2 = (bf16[5120]{0:T(1024)(128)(2,1)S(1)}, bf16[5120]{0:T(1024)(128)(2,1)}, u32[]{:S(2)}) copy-start(bf16[5120]{0:T(1024)(128)(2,1)} %param.16) | copy-start | bytes 30724
  5.0 10.6 %copy-start = (bf16[5120]{0:T(1024)(128)(2,1)S(1)}, bf16[5120]{0:T(1024)(128)(2,1)}, u32[]{:S(2)}) copy-start(bf16[5120]{0:T(1024)(128)(2,1)} %refs_5_.7) | copy-start | bytes 30724
  9.6 60.2 %collective-permute-start.1 = (bf16[2,128,5120]{2,1,0:T(8,128)(2,1)}, bf16[2,128,5120]{2,1,0:T(8,128)(2,1)}, u32[]{:S(2)}, u32[]{:S(2)}) collective-permute-start(bf16[2,128,5120]{2,1,0:T(8,128)(2,1)} %get-tuple-element.45), channel_id=1, source_target_pairs={{0,3},{1,2},{2,1},{3,0},{4,7},{5,6},{6,5},{7,4},{8,11},{9,10},{10,... | collective-permute-start | bytes 7864328 | tf_op jit(solution)/shard_map/ppermute | solution.py:351
  12.2 114.0 %collective-permute-start = (bf16[2,128,5120]{2,1,0:T(8,128)(2,1)S(1)}, bf16[2,128,5120]{2,1,0:T(8,128)(2,1)}, u32[]{:S(2)}, u32[]{:S(2)}) collective-permute-start(bf16[2,128,5120]{2,1,0:T(8,128)(2,1)S(1)} %get-tuple-element.46), channel_id=1, source_target_pairs={{0,2},{1,3},{2,0},{3,1},{4,6},{5,7},{6,4},{7,5},{8,10},{9,11},{10,... | collective-permute-start | bytes 7864328 | tf_op jit(solution)/shard_map/ppermute | solution.py:351
  12.2 249.1 %collective-permute-start.5 = (s32[3,128]{1,0:T(4,128)S(1)}, s32[3,128]{1,0:T(4,128)S(1)}, u32[]{:S(2)}, u32[]{:S(2)}) collective-permute-start(s32[3,128]{1,0:T(4,128)S(1)} %get-tuple-element.56), channel_id=1, source_target_pairs={{0,3},{1,2},{2,1},{3,0},{4,7},{5,6},{6,5},{7,4},{8,11},{9,10},{10,... | collective-permute-start | bytes 4616 | tf_op jit(solution)/shard_map/ppermute | solution.py:351
  13.6 247.7 %collective-permute-start.3 = (s32[3,128]{1,0:T(4,128)S(1)}, s32[3,128]{1,0:T(4,128)S(1)}, u32[]{:S(2)}, u32[]{:S(2)}) collective-permute-start(s32[3,128]{1,0:T(4,128)S(1)} %get-tuple-element.57), channel_id=1, source_target_pairs={{0,1},{1,0},{2,3},{3,2},{4,5},{5,4},{6,7},{7,6},{8,9},{9,8},{10,11... | collective-permute-start | bytes 4616 | tf_op jit(solution)/shard_map/ppermute | solution.py:351
  69.8 191.5 %collective-permute-start.4 = (s32[3,128]{1,0:T(4,128)S(1)}, s32[3,128]{1,0:T(4,128)S(1)}, u32[]{:S(2)}, u32[]{:S(2)}) collective-permute-start(s32[3,128]{1,0:T(4,128)S(1)} %get-tuple-element.59), channel_id=1, source_target_pairs={{0,2},{1,3},{2,0},{3,1},{4,6},{5,7},{6,4},{7,5},{8,10},{9,11},{10,... | collective-permute-start | bytes 4616 | tf_op jit(solution)/shard_map/ppermute | solution.py:351
  126.2 331.8 %collective-permute-start.6 = (bf16[1,128,5120]{2,1,0:T(8,128)(2,1)}, bf16[1,128,5120]{2,1,0:T(8,128)(2,1)}, u32[]{:S(2)}, u32[]{:S(2)}) collective-permute-start(bf16[1,128,5120]{2,1,0:T(8,128)(2,1)} %get-tuple-element.35), channel_id=1, source_target_pairs={{0,2},{1,3},{2,0},{3,1},{4,6},{5,7},{6,4},{7,5},{8,10},{9,11},{10,... | collective-permute-start | bytes 3932168 | tf_op jit(solution)/shard_map/ppermute | solution.py:351
  127.8 330.1 %collective-permute-start.7 = (bf16[1,128,5120]{2,1,0:T(8,128)(2,1)}, bf16[1,128,5120]{2,1,0:T(8,128)(2,1)}, u32[]{:S(2)}, u32[]{:S(2)}) collective-permute-start(bf16[1,128,5120]{2,1,0:T(8,128)(2,1)} %get-tuple-element.36), channel_id=1, source_target_pairs={{0,3},{1,2},{2,1},{3,0},{4,7},{5,6},{6,5},{7,4},{8,11},{9,10},{10,... | collective-permute-start | bytes 3932168 | tf_op jit(solution)/shard_map/ppermute | solution.py:351
  455.9 120.4 %collective-permute-start.9 = (bf16[2,128,5120]{2,1,0:T(8,128)(2,1)}, bf16[2,128,5120]{2,1,0:T(8,128)(2,1)}, u32[]{:S(2)}, u32[]{:S(2)}) collective-permute-start(bf16[2,128,5120]{2,1,0:T(8,128)(2,1)} %get-tuple-element.40), channel_id=1, source_target_pairs={{0,3},{1,2},{2,1},{3,0},{4,7},{5,6},{6,5},{7,4},{8,11},{9,10},{10,... | collective-permute-start | bytes 7864328 | tf_op jit(solution)/shard_map/ppermute | solution.py:351
  457.6 118.6 %collective-permute-start.8 = (bf16[2,128,5120]{2,1,0:T(8,128)(2,1)}, bf16[2,128,5120]{2,1,0:T(8,128)(2,1)}, u32[]{:S(2)}, u32[]{:S(2)}) collective-permute-start(bf16[2,128,5120]{2,1,0:T(8,128)(2,1)} %get-tuple-element.37.refs_5_), channel_id=1, source_target_pairs={{0,2},{1,3},{2,0},{3,1},{4,6},{5,7},{6,4},{7,5},{8,10},{9,11},{10,... | collective-permute-start | bytes 7864328 | tf_op jit(solution)/shard_map/ppermute | solution.py:351
  631.1 7.0 %collective-permute-start.10 = (bf16[3,128,5120]{2,1,0:T(8,128)(2,1)}, bf16[3,128,5120]{2,1,0:T(8,128)(2,1)S(1)}, u32[]{:S(2)}, u32[]{:S(2)}) collective-permute-start(bf16[3,128,5120]{2,1,0:T(8,128)(2,1)} %get-tuple-element.43), channel_id=1, source_target_pairs={{0,1},{1,0},{2,3},{3,2},{4,5},{5,4},{6,7},{7,6},{8,9},{9,8},{10,11... | collective-permute-start | bytes 11796488 | tf_op jit(solution)/shard_map/ppermute | solution.py:351
  631.2 31.9 %collective-permute-start.11 = (bf16[1,128,5120]{2,1,0:T(8,128)(2,1)}, bf16[1,128,5120]{2,1,0:T(8,128)(2,1)S(1)}, u32[]{:S(2)}, u32[]{:S(2)}) collective-permute-start(bf16[1,128,5120]{2,1,0:T(8,128)(2,1)} %get-tuple-element.41.refs_8_), channel_id=1, source_target_pairs={{0,2},{1,3},{2,0},{3,1},{4,6},{5,7},{6,4},{7,5},{8,10},{9,11},{10,... | collective-permute-start | bytes 3932168 | tf_op jit(solution)/shard_map/ppermute | solution.py:351
  632.9 57.2 %collective-permute-start.12 = (bf16[1,128,5120]{2,1,0:T(8,128)(2,1)}, bf16[1,128,5120]{2,1,0:T(8,128)(2,1)S(1)}, u32[]{:S(2)}, u32[]{:S(2)}) collective-permute-start(bf16[1,128,5120]{2,1,0:T(8,128)(2,1)} %get-tuple-element.44), channel_id=1, source_target_pairs={{0,3},{1,2},{2,1},{3,0},{4,7},{5,6},{6,5},{7,4},{8,11},{9,10},{10,... | collective-permute-start | bytes 3932168 | tf_op jit(solution)/shard_map/ppermute | solution.py:351

commit v2 on v1

--- a/solution.py
+++ b/solution.py
@@ -13,7 +13,7 @@
 NORM_EPS = 1e-6
 SCALE = HEAD_DIM ** -0.5
 LOG2E = 1.4426950408889634
-QKV_TILE = 1024
+QKV_TILE = 1280
 OUT_TILE = 512
 HEADS_PER_STEP = 4
 VMEM_BYTES = 63 * 2 ** 20
@@ -23,7 +23,11 @@
     inv_freq = 1.0 / (ROPE_THETA ** (jnp.arange(0, HEAD_DIM, 2, dtype=jnp.float32) / HEAD_DIM))
     angles = pos_ids.astype(jnp.float32)[..., None] * inv_freq
     cos_t, sin_t = jnp.cos(angles), jnp.sin(angles)
-    return jnp.concatenate([cos_t, cos_t], axis=-1), jnp.concatenate([-sin_t, sin_t], axis=-1)
+    return cos_t, sin_t
+
+
+def pair_heads(gain):
+    return gain.reshape(-1, 2, 2, HEAD_DIM // 2).transpose(0, 2, 1, 3).reshape(1, -1)
 
 
 def lane_sums(sq):
@@ -35,6 +39,38 @@
 
 def row_copies(srcs, dst, sems):
     return [pltpu.make_async_copy(src, dst.at[pl.ds(i * 128, 128), :], sems.at[i]) for i, src in enumerate(srcs)]
+
+
+def pick_kernel(takes, per_dev, x_ref, *refs):
+    outs, (buf, sem_in, sem_out) = refs[:len(takes)], refs[len(takes):]
+    dev = lax.axis_index('sp')
+    loads, stores = [], []
+    for (r, first, count), out in zip(takes, outs):
+        base = jnp.bitwise_xor(dev, r) * per_dev + first
+        for b in range(count):
+            i = len(loads)
+            loads.append(pltpu.make_async_copy(x_ref.at[base + b], buf.at[i], sem_in.at[i]))
+            stores.append(pltpu.make_async_copy(buf.at[i], out.at[b], sem_out.at[i]))
+    for cp in loads:
+        cp.start()
+    for load, store in zip(loads, stores):
+        load.wait()
+        store.start()
+    for cp in stores:
+        cp.wait()
+
+
+def pick_call(x_loc, takes, per_dev):
+    n_total = sum(t[2] for t in takes)
+    any_spec = pl.BlockSpec(memory_space=pl.ANY)
+    return pl.pallas_call(
+        functools.partial(pick_kernel, takes, per_dev),
+        in_specs=[any_spec],
+        out_specs=[any_spec] * len(takes),
+        out_shape=[jax.ShapeDtypeStruct((t[2],) + x_loc.shape[1:], x_loc.dtype) for t in takes],
+        scratch_shapes=[pltpu.VMEM((n_total,) + x_loc.shape[1:], x_loc.dtype)] + [pltpu.SemaphoreType.DMA((n_total,))] * 2,
+        compiler_params=pltpu.CompilerParams(vmem_limit_bytes=VMEM_BYTES),
+    )(x_loc)
 
 
 def qkv_kernel(n_tiles, own, counts, aliased, *refs):
@@ -43,6 +79,7 @@
     weights = refs[n_pieces:n_pieces + 3]
     qkv_out, stat_out, x_buf, w_buf, x_sem, w_sem = refs[n_pieces + 4 + 2 * aliased:]
     step = pl.program_id(0)
+    rows = sum(counts) * 128
     slot = lax.rem(step, 2)
 
     def fetch(at_step):
@@ -71,10 +108,22 @@
         fetch(step + 1)
 
     pltpu.make_async_copy(weights[0].at[:, pl.ds(0, QKV_TILE)], w_buf.at[slot], w_sem.at[slot]).wait()
-    proj = jnp.dot(x_buf[...], w_buf[slot], preferred_element_type=jnp.float32).astype(jnp.bfloat16)
-    qkv_out[...] = proj.reshape(qkv_out.shape)
-    wide = proj.astype(jnp.float32)
-    part = lane_sums(wide * wide).reshape(stat_out.shape)
+    proj = jnp.dot(x_buf[...], w_buf[slot], preferred_element_type=jnp.float32)
+    plain = step >= 2 * n_tiles
+    low = lax.broadcasted_iota(jnp.int32, (rows, 128), 1) < 64
+    keep_even = jnp.logical_or(low, plain)
+    keep_odd = jnp.logical_not(jnp.logical_and(low, jnp.logical_not(plain)))
+    part = None
+    for pair in range(QKV_TILE // 256):
+        cols = slice(pair * 256, pair * 256 + 128), slice(pair * 256 + 128, pair * 256 + 256)
+        even, odd = (proj[:, c].astype(jnp.bfloat16) for c in cols)
+        moved = pltpu.roll(jnp.where(low, odd, even), 64, 1)
+        for c, val in zip(cols, (jnp.where(keep_even, even, moved), jnp.where(keep_odd, odd, moved))):
+            qkv_out[0, :, :, :, c] = val.reshape(qkv_out.shape[1:4] + (128,))
+        even, odd = even.astype(jnp.float32), odd.astype(jnp.float32)
+        sq = even * even + odd * odd
+        part = sq if part is None else part + sq
+    part = part.reshape(stat_out.shape)
     first = lax.rem(step, n_tiles) == 0
 
     @pl.when(first)
@@ -122,8 +171,9 @@
                 rows = slice(j * 128, (j + 1) * 128)
                 total = jnp.sum(stat_refs[j][which, 0, 0], axis=-1, keepdims=True)
                 inv = lax.rsqrt(total * (1.0 / width) + NORM_EPS)
-                cos_n[which, rows, :] = cos_ref[0, rows, :] * inv
-                sin_n[which, rows, :] = sin_ref[0, rows, :] * inv
+                cos_v, sin_v = cos_ref[0, rows, :], sin_ref[0, rows, :]
+                cos_n[which, rows, :] = jnp.concatenate([cos_v, cos_v], axis=1) * inv
+                sin_n[which, rows, :] = jnp.concatenate([sin_v, sin_v], axis=1) * inv
 
     row_id = lax.broadcasted_iota(jnp.int32, (128, 128), 0)
     col_id = lax.broadcasted_iota(jnp.int32, (128, 128), 1)
@@ -134,19 +184,32 @@
     def scores(q, k):
         return lax.dot_general(q, k, (((1,), (1,)), ((), ())), preferred_element_type=jnp.float32)
 
-    def prepare(h):
-        lanes = slice(h * 128, (h + 1) * 128)
-        parts = ([], [])
+    low = lax.broadcasted_iota(jnp.int32, (512, 128), 1) < 64
+    nothing = jnp.zeros((512, 128), jnp.bfloat16)
+
+    def prepare(pair):
+        sides = []
         for which, gain_ref in ((0, gq_ref), (1, gk_ref)):
-            gain = gain_ref[:, lanes].astype(jnp.float32)
+            halves = []
+            for half in range(2):
+                lanes = slice(pair * 256 + half * 128, pair * 256 + half * 128 + 128)
+                gain = gain_ref[:, lanes].astype(jnp.float32)
+                halves.append([qkv_refs[j][which, 0, 0, :, lanes].astype(jnp.float32) * gain for j in range(4)])
+            rot = ([], [])
             for j in range(4):
                 rows = slice(j * 128, (j + 1) * 128)
-                u = qkv_refs[j][which, 0, 0, :, lanes].astype(jnp.float32) * gain
-                rot = u * cos_n[which, rows, :] + pltpu.roll(u, 64, 1) * sin_n[which, rows, :]
-                parts[which].append(rot.astype(jnp.bfloat16))
-        q, k = parts
-        k_lo, k_hi = jnp.concatenate(k[:2], axis=0), jnp.concatenate(k[2:], axis=0)
-        return scores(jnp.concatenate(q, axis=0), k_lo), scores(jnp.concatenate(q[2:], axis=0), k_hi)
+                cos_v, sin_v = cos_n[which, rows, :], sin_n[which, rows, :]
+                first, second = halves[0][j], halves[1][j]
+                rot[0].append((first * cos_v - second * sin_v).astype(jnp.bfloat16))
+                rot[1].append((second * cos_v + first * sin_v).astype(jnp.bfloat16))
+            sides.append([jnp.concatenate(r, axis=0) for r in rot])
+        q = jnp.concatenate(sides[0], axis=1)
+        out = []
+        for head in range(2):
+            k = jnp.concatenate([jnp.where(low, k_half, nothing) if head == 0 else jnp.where(low, nothing, k_half)
+                                 for k_half in sides[1]], axis=1)
+            out.append((scores(q, k[:256]), scores(q[256:], k[256:])))
+        return out
 
     def finish(h, s_lo, s_hi):
         lanes = slice(h * 128, (h + 1) * 128)
@@ -175,9 +238,10 @@
             out_ref[jnp.bitwise_xor(dev, j), 0, :, lanes] = o.astype(jnp.bfloat16)
 
     ready = prepare(0)
-    for h in range(HEADS_PER_STEP):
-        following = prepare(h + 1) if h + 1 < HEADS_PER_STEP else None
-        finish(h, *ready)
+    for pair in range(HEADS_PER_STEP // 2):
+        following = prepare(pair + 1) if pair + 1 < HEADS_PER_STEP // 2 else None
+        for head in range(2):
+            finish(2 * pair + head, *ready[head])
         ready = following
 
 
@@ -191,7 +255,7 @@
     def stat_map(j):
         return lambda b, h, dev_ref: (0, jnp.bitwise_xor(dev_ref[0], j), b + first, 0, 0)
 
-    table_spec = pl.BlockSpec((1, 512, 128), lambda b, h, dev_ref: (b + first, 0, 0))
+    table_spec = pl.BlockSpec((1, 512, HEAD_DIM // 2), lambda b, h, dev_ref: (b + first, 0, 0))
     gain_spec = pl.BlockSpec((1, cols), lambda b, h, dev_ref: (0, h))
     n_heads = width // 128
     return pl.pallas_call(
@@ -208,7 +272,7 @@
         compiler_params=pltpu.CompilerParams(vmem_limit_bytes=VMEM_BYTES, dimension_semantics=("arbitrary", "arbitrary")),
         cost_estimate=pl.CostEstimate(flops=n_batch * n_heads * 512 * 512 * 128 * 8, transcendentals=0,
                                       bytes_accessed=n_batch * 512 * width * 8),
-    )(dev, *[qkv] * 4, *[stats] * 4, cos_t, sin_t, gain_q.reshape(1, width), gain_k.reshape(1, width))
+    )(dev, *[qkv] * 4, *[stats] * 4, cos_t, sin_t, pair_heads(gain_q), pair_heads(gain_k))
 
 
 def out_kernel(n_tiles, rel, o_counts, x_counts, own, moved, *refs):
@@ -350,11 +414,10 @@
         def swap(arr, r):
             return lax.ppermute(arr, 'sp', [(i, i ^ r) for i in range(4)])
 
-        def piece(r, first, count):
-            return lax.dynamic_slice_in_dim(x_loc, (dev ^ r) * per_dev + first, count, axis=0)
-
-        x_far01 = [swap(piece(r, 0, 2), r) for r in (2, 3)]
-        x_near = swap(piece(1, 0, per_dev), 1)
+        for_near, = pick_call(x_loc, ((1, 0, per_dev),), per_dev)
+        x_near = swap(for_near, 1)
+        p01_2, p01_3, p2, p3 = pick_call(x_loc, ((2, 0, 2), (3, 0, 2), (2, 2, 1), (3, 2, 1)), per_dev)
+        x_far01 = [swap(p01_2, 2), swap(p01_3, 3)]
         pos_parts = [lax.dynamic_slice_in_dim(pos_loc, dev * per_dev, per_dev, axis=0)]
         for r in range(1, 4):
             pos_parts.append(swap(lax.dynamic_slice_in_dim(pos_loc, (dev ^ r) * per_dev, per_dev, axis=0), r))
@@ -362,7 +425,7 @@
         weights = (w_query, w_key, w_value)
         dev_arr = jnp.full((1,), dev, jnp.int32)
         near = qkv_call([x_loc, x_near], (per_dev, per_dev), True, weights, per_dev, 0, 0, (), gain_q)
-        p2, p3, x_far01[0], x_far01[1] = lax.optimization_barrier((piece(2, 2, 1), piece(3, 2, 1), x_far01[0], x_far01[1]))
+        p2, p3, x_far01[0], x_far01[1] = lax.optimization_barrier((p2, p3, x_far01[0], x_far01[1]))
         x_far2 = [swap(p2, 2), swap(p3, 3)]
         qkv01, stats01 = qkv_call(x_far01, (2, 2), False, weights, per_dev, 1, 0, near, gain_q)
         pos_parts, _ = lax.optimization_barrier((pos_parts, near[1]))
@@ -383,9 +446,9 @@
         def put(acc, part, r, first):
             return lax.dynamic_update_slice_in_dim(acc, part, (dev ^ r) * per_dev + first, axis=0)
 
-        y_all = put(y_all, z_near, 1, 0)
         y_all = put(y_all, z_far2[0], 2, 2)
         y_all = put(y_all, z_far2[1], 3, 2)
+        y_all = put(y_all, z_near, 1, 0)
         return y_all
 
     tok_spec = P('dp', 'sp', None)

time: 692 us -> 673 us (0.973)
  Pallas kernels: 497 us -> 475 us
  waiting for transfers between devices: 159 us -> 170 us
  local copies, waits for them, and re-layouts: 18.6 us -> 8.82 us
    pallas_call x2, Pallas kernels: 89.6 us -> 56.9 us  [attention_call(): pl.pallas_call(functools.partial(attention_kernel, width), grid_spec=pltp...]
    dynamic_slice x3 -> x0, local copies, waits for them, and re-layouts: 12.2 us -> none  [piece(): lax.dynamic_slice_in_dim(x_loc, (dev ^ r) * per_dev + first, count, axis=0)]
    ppermute x13, waiting for transfers between devices: 159 us -> 170 us  [swap(): return lax.ppermute(arr, 'sp', [(i, i ^ r) for i in range(4)])]
    pallas_call x0 -> x2, Pallas kernels: none -> 9.62 us  [pick_call(): pl.pallas_call(functools.partial(pick_kernel, takes, per_dev), in_specs=[...]
  transfers between devices with their start and end apart: 13 -> 13, of which waited for: 5 -> 5; matrix products, arithmetic and copies ran while one was open for 3% -> 1% of each run, Pallas kernels for 64% -> 62%
where the time goes in v2:
time: 673 us; the launch traced here: 672 us
  Pallas kernels  475 us (71%)
  waiting for transfers between devices  170 us (25%)
  starting transfers between devices  13.1 us (2%)
  local copies, waits for them, and re-layouts  8.82 us (1%)
    pallas_call x3, Pallas kernels, qkv_call(): pl.pallas_call(functools.partial(qkv_kernel, n_tiles, own, counts, bool(p...  287 us
    ppermute x13, waiting for transfers between devices, swap(): return lax.ppermute(arr, 'sp', [(i, i ^ r) for i in range(4)])  170 us
    pallas_call x3, Pallas kernels, out_call(): pl.pallas_call(functools.partial(out_kernel, n_tiles, rel, o_counts, x_co...  122 us
    pallas_call x2, Pallas kernels, attention_call(): pl.pallas_call(functools.partial(attention_kernel, width), grid_spec=pltp...  56.9 us
  transfers between devices with their start and end apart: 13, of which 5 were waited for; matrix products, arithmetic and copies ran while one was open for 1% of the time, Pallas kernels for 62%

profile of v2, /device:TPU:0, one launch (start us, length us, event | category | flops | bytes accessed | tf_op | source)
XLA Modules:
  0.0 672.1 jit_solution(4642710485442542441)
XLA Ops:
  0.0 3.3 shard_map.92
  3.3 0.0 copy-start.3
  3.3 0.0 copy-start.1
  3.3 0.0 copy-start.2
  3.3 0.0 copy-start
  3.3 0.8 collective-permute-start.2
  4.1 6.3 shard_map.91
  10.4 2.5 collective-permute-start
  13.0 0.1 collective-permute-start.1
  13.1 0.0 copy-done.3
  13.1 1.6 collective-permute-start.5
  14.8 0.2 collective-permute-start.3
  15.0 0.0 copy-done.1
  15.0 0.6 reshape.64.refs_4_.refs_7_
  15.6 0.0 copy-done.2
  15.6 0.1 reshape.62
  15.7 0.7 reshape.63.refs_11_
  16.4 0.0 copy-done
  16.4 0.1 reshape.60
  16.5 0.7 reshape.61.refs_10_
  17.2 53.8 %collective-permute-done.refs_0_.refs_1_ = bf16[2,128,5120]{2,1,0:T(8,128)(2,1)} collective-permute-done((bf16[2,128,5120]{2,1,0:T(8,128)(2,1)}, bf16[2,128,5120]{2,1,0:T(8,128)(2,1)}, u32[]{:S(2)}, u32[]{:S(2)}) %collective-permute-start) | collective-permute-done | bytes 2621472 | tf_op jit(solution)/shard_map/ppermute | solution.py:415
  71.0 2.0 collective-permute-start.4
  73.0 53.7 %collective-permute-done.1.refs_1_.refs_2_ = bf16[2,128,5120]{2,1,0:T(8,128)(2,1)} collective-permute-done((bf16[2,128,5120]{2,1,0:T(8,128)(2,1)}, bf16[2,128,5120]{2,1,0:T(8,128)(2,1)}, u32[]{:S(2)}, u32[]{:S(2)}) %collective-permute-start.1) | collective-permute-done | bytes 2621472 | tf_op jit(solution)/shard_map/ppermute | solution.py:415
  126.8 1.5 collective-permute-start.6
  128.2 0.0 collective-permute-done.2.refs_1_.refs_3_
  128.2 0.0 collective-permute-start.7
  128.2 135.0 %shard_map.93 = (bf16[3,4,3,128,5120]{4,3,2,1,0:T(8,128)(2,1)}, f32[3,4,3,128,128]{4,3,2,1,0:T(8,128)}) custom-call(bf16[12,128,5120]{2,1,0:T(8,128)(2,1)} %refs_2_.7, bf16[3,128,5120]{2,1,0:T(8,128)(2,1)} %collective-permute-done.2.refs_1_.refs_3_, bf16[5120,5120]{1,0:T(8,128)(2,1)} %refs_2_.6, bf16[5120,5120]{1,0:T(8,128)(2,1)} %refs_3_.8, ...), custom_call_target="tpu_custom_call" | custom-call | flops 120795955200 | bytes 157286400 | tf_op jit(solution)/shard_map/pallas_call | solution.py:145
  263.3 0.0 collective-permute-done.5
  263.3 0.0 collective-permute-done.3
  263.3 0.0 collective-permute-done.4
  263.3 4.3 multiply_sine_fusion
  267.7 93.0 %shard_map.94 = (bf16[3,4,3,128,5120]{4,3,2,1,0:T(8,128)(2,1)}, f32[3,4,3,128,128]{4,3,2,1,0:T(8,128)}) custom-call(bf16[2,128,5120]{2,1,0:T(8,128)(2,1)} %collective-permute-done.refs_0_.refs_1_, bf16[2,128,5120]{2,1,0:T(8,128)(2,1)} %collective-permute-done.1.refs_1_.refs_2_, ...), custom_call_target="tpu_custom_call", output_to_operand_aliasing={{0}: (6, {}), {1}: (7, {})} | custom-call | flops 80530636800 | bytes 157286400 | tf_op jit(solution)/shard_map/pallas_call | solution.py:145
  360.6 37.6 %shard_map.95.refs_0_ = bf16[4,2,128,5120]{3,2,1,0:T(8,128)(2,1)} custom-call(s32[1]{0:T(128)} %bitcast.dev_ref, bf16[3,4,3,128,5120]{4,3,2,1,0:T(8,128)(2,1)} %get-tuple-element.37.refs_0_.refs_1_.refs_2_.refs_3_.refs_6_, bf16[3,4,3,128,5120]{4,3,2,1,0:T(8,128)(2,1)} %get-tuple-element.37.refs_0_.refs_1_.refs_2_.refs_3_.refs_6_, ...), custom_call_target="tpu_custom_call" | custom-call | flops 21474836480 | bytes 41943040 | tf_op jit(solution)/shard_map/pallas_call | solution.py:261
  398.2 39.1 %shard_map.96 = (bf16[2,128,5120]{2,1,0:T(8,128)(2,1)}, bf16[2,128,5120]{2,1,0:T(8,128)(2,1)}) custom-call(bf16[4,2,128,5120]{3,2,1,0:T(8,128)(2,1)} %shard_map.95.refs_0_, bf16[2,128,5120]{2,1,0:T(8,128)(2,1)} %collective-permute-done.refs_0_.refs_1_, bf16[2,128,5120]{2,1,0:T(8,128)(2,1)} %collective-permute-done.1.refs_1_.refs_2_, ...), custom_call_target="tpu_custom_call" | custom-call | flops 26843545600 | bytes 52428800 | tf_op jit(solution)/shard_map/pallas_call | solution.py:392
  437.3 1.7 collective-permute-start.9
  438.9 0.8 collective-permute-start.8
  439.7 0.0 collective-permute-done.6.refs_0_.refs_1_
  439.7 0.0 collective-permute-done.7.refs_1_.refs_2_
  439.7 59.3 %shard_map.97 = (bf16[3,4,3,128,5120]{4,3,2,1,0:T(8,128)(2,1)}, f32[3,4,3,128,128]{4,3,2,1,0:T(8,128)}) custom-call(bf16[1,128,5120]{2,1,0:T(8,128)(2,1)} %collective-permute-done.6.refs_0_.refs_1_, bf16[1,128,5120]{2,1,0:T(8,128)(2,1)} %collective-permute-done.7.refs_1_.refs_2_, ...), custom_call_target="tpu_custom_call", output_to_operand_aliasing={{0}: (6, {}), {1}: (7, {})} | custom-call | flops 40265318400 | bytes 157286400 | tf_op jit(solution)/shard_map/pallas_call | solution.py:145
  499.0 19.3 %shard_map.98.refs_0_.refs_1_ = bf16[4,1,128,5120]{3,2,1,0:T(8,128)(2,1)} custom-call(s32[1]{0:T(128)} %bitcast.dev_ref, bf16[3,4,3,128,5120]{4,3,2,1,0:T(8,128)(2,1)} %get-tuple-element.46.refs_0_.refs_1_.refs_2_.refs_3_, bf16[3,4,3,128,5120]{4,3,2,1,0:T(8,128)(2,1)} %get-tuple-element.46.refs_0_.refs_1_.refs_2_.refs_3_, ...), custom_call_target="tpu_custom_call" | custom-call | flops 10737418240 | bytes 20971520 | tf_op jit(solution)/shard_map/pallas_call | solution.py:261
  518.3 28.0 %shard_map.99 = (bf16[1,128,5120]{2,1,0:T(8,128)(2,1)}, bf16[1,128,5120]{2,1,0:T(8,128)(2,1)}) custom-call(bf16[4,1,128,5120]{3,2,1,0:T(8,128)(2,1)} %shard_map.98.refs_0_.refs_1_, bf16[1,128,5120]{2,1,0:T(8,128)(2,1)} %collective-permute-done.6.refs_0_.refs_1_, bf16[1,128,5120]{2,1,0:T(8,128)(2,1)} %collective-permute-done.7.refs_1_.refs_2_, ...), custom_call_target="tpu_custom_call" | custom-call | flops 13421772800 | bytes 52428800 | tf_op jit(solution)/shard_map/pallas_call | solution.py:392
  546.3 0.0 collective-permute-done.9.refs_5_
  546.3 6.7 collective-permute-done.8.refs_4_
  553.0 54.7 %shard_map.100 = (bf16[12,128,5120]{2,1,0:T(8,128)(2,1)}, bf16[3,128,5120]{2,1,0:T(8,128)(2,1)}) custom-call(bf16[4,2,128,5120]{3,2,1,0:T(8,128)(2,1)} %shard_map.95.refs_0_, bf16[4,1,128,5120]{3,2,1,0:T(8,128)(2,1)} %shard_map.98.refs_0_.refs_1_, bf16[12,128,5120]{2,1,0:T(8,128)(2,1)} %refs_2_.7, ...), custom_call_target="tpu_custom_call" | custom-call | flops 40265318400 | bytes 52428800 | tf_op jit(solution)/shard_map/pallas_call | solution.py:392
  607.6 0.0 collective-permute-start.12
  607.7 1.6 collective-permute-start.10
  609.3 0.2 collective-permute-start.11
  609.5 30.0 %collective-permute-done.10 = bf16[1,128,5120]{2,1,0:T(8,128)(2,1)S(1)} collective-permute-done((bf16[1,128,5120]{2,1,0:T(8,128)(2,1)}, bf16[1,128,5120]{2,1,0:T(8,128)(2,1)S(1)}, u32[]{:S(2)}, u32[]{:S(2)}) %collective-permute-start.10) | collective-permute-done | bytes 1310752 | tf_op jit(solution)/shard_map/ppermute | solution.py:415
  639.6 1.1 constant_dynamic-update-slice_fusion.2
  640.7 25.9 %collective-permute-done.11 = bf16[1,128,5120]{2,1,0:T(8,128)(2,1)S(1)} collective-permute-done((bf16[1,128,5120]{2,1,0:T(8,128)(2,1)}, bf16[1,128,5120]{2,1,0:T(8,128)(2,1)S(1)}, u32[]{:S(2)}, u32[]{:S(2)}) %collective-permute-start.11) | collective-permute-done | bytes 1310752 | tf_op jit(solution)/shard_map/ppermute | solution.py:415
  666.7 1.1 constant_dynamic-update-slice_fusion.1
  667.8 0.0 collective-permute-done.12
  667.8 4.3 constant_dynamic-update-slice_fusion
  (7 shorter events, 0.1 us)
Async XLA Ops:
  3.3 9.8 %copy-start.3 = (s32[12,128]{1,0:T(8,128)S(1)}, s32[12,128]{1,0:T(8,128)}, u32[]{:S(2)}) copy-start(s32[12,128]{1,0:T(8,128)} %param.10) | copy-start | bytes 18436
  3.3 11.7 %copy-start.1 = (bf16[5120]{0:T(1024)(128)(2,1)S(1)}, bf16[5120]{0:T(1024)(128)(2,1)}, u32[]{:S(2)}) copy-start(bf16[5120]{0:T(1024)(128)(2,1)} %param.17) | copy-start | bytes 30724
  3.3 12.3 %copy-start.2 = (bf16[5120]{0:T(1024)(128)(2,1)S(1)}, bf16[5120]{0:T(1024)(128)(2,1)}, u32[]{:S(2)}) copy-start(bf16[5120]{0:T(1024)(128)(2,1)} %param.16) | copy-start | bytes 30724
  3.3 13.1 %copy-start = (bf16[5120]{0:T(1024)(128)(2,1)S(1)}, bf16[5120]{0:T(1024)(128)(2,1)}, u32[]{:S(2)}) copy-start(bf16[5120]{0:T(1024)(128)(2,1)} %refs_5_.7) | copy-start | bytes 30724
  3.3 124.9 %collective-permute-start.2 = (bf16[3,128,5120]{2,1,0:T(8,128)(2,1)}, bf16[3,128,5120]{2,1,0:T(8,128)(2,1)}, u32[]{:S(2)}, u32[]{:S(2)}) collective-permute-start(bf16[3,128,5120]{2,1,0:T(8,128)(2,1)} %shard_map.92), channel_id=1, source_target_pairs={{0,1},{1,0},{2,3},{3,2},{4,5},{5,4},{6,7},{7,6},{8,9},{9,8},{10,11... | collective-permute-start | bytes 11796488 | tf_op jit(solution)/shard_map/ppermute | solution.py:415
  10.4 60.6 %collective-permute-start = (bf16[2,128,5120]{2,1,0:T(8,128)(2,1)}, bf16[2,128,5120]{2,1,0:T(8,128)(2,1)}, u32[]{:S(2)}, u32[]{:S(2)}) collective-permute-start(bf16[2,128,5120]{2,1,0:T(8,128)(2,1)} %get-tuple-element.31), channel_id=1, source_target_pairs={{0,2},{1,3},{2,0},{3,1},{4,6},{5,7},{6,4},{7,5},{8,10},{9,11},{10,... | collective-permute-start | bytes 7864328 | tf_op jit(solution)/shard_map/ppermute | solution.py:415
  13.0 113.8 %collective-permute-start.1 = (bf16[2,128,5120]{2,1,0:T(8,128)(2,1)}, bf16[2,128,5120]{2,1,0:T(8,128)(2,1)}, u32[]{:S(2)}, u32[]{:S(2)}) collective-permute-start(bf16[2,128,5120]{2,1,0:T(8,128)(2,1)} %get-tuple-element.32), channel_id=1, source_target_pairs={{0,3},{1,2},{2,1},{3,0},{4,7},{5,6},{6,5},{7,4},{8,11},{9,10},{10,... | collective-permute-start | bytes 7864328 | tf_op jit(solution)/shard_map/ppermute | solution.py:415
  13.1 250.1 %collective-permute-start.5 = (s32[3,128]{1,0:T(4,128)S(1)}, s32[3,128]{1,0:T(4,128)S(1)}, u32[]{:S(2)}, u32[]{:S(2)}) collective-permute-start(s32[3,128]{1,0:T(4,128)S(1)} %get-tuple-element.59), channel_id=1, source_target_pairs={{0,3},{1,2},{2,1},{3,0},{4,7},{5,6},{6,5},{7,4},{8,11},{9,10},{10,... | collective-permute-start | bytes 4616 | tf_op jit(solution)/shard_map/ppermute | solution.py:415
  14.8 248.5 %collective-permute-start.3 = (s32[3,128]{1,0:T(4,128)S(1)}, s32[3,128]{1,0:T(4,128)S(1)}, u32[]{:S(2)}, u32[]{:S(2)}) collective-permute-start(s32[3,128]{1,0:T(4,128)S(1)} %get-tuple-element.60), channel_id=1, source_target_pairs={{0,1},{1,0},{2,3},{3,2},{4,5},{5,4},{6,7},{7,6},{8,9},{9,8},{10,11... | collective-permute-start | bytes 4616 | tf_op jit(solution)/shard_map/ppermute | solution.py:415
  71.0 192.3 %collective-permute-start.4 = (s32[3,128]{1,0:T(4,128)S(1)}, s32[3,128]{1,0:T(4,128)S(1)}, u32[]{:S(2)}, u32[]{:S(2)}) collective-permute-start(s32[3,128]{1,0:T(4,128)S(1)} %get-tuple-element.62), channel_id=1, source_target_pairs={{0,2},{1,3},{2,0},{3,1},{4,6},{5,7},{6,4},{7,5},{8,10},{9,11},{10,... | collective-permute-start | bytes 4616 | tf_op jit(solution)/shard_map/ppermute | solution.py:415
  126.8 312.9 %collective-permute-start.6 = (bf16[1,128,5120]{2,1,0:T(8,128)(2,1)}, bf16[1,128,5120]{2,1,0:T(8,128)(2,1)}, u32[]{:S(2)}, u32[]{:S(2)}) collective-permute-start(bf16[1,128,5120]{2,1,0:T(8,128)(2,1)} %get-tuple-element.43), channel_id=1, source_target_pairs={{0,2},{1,3},{2,0},{3,1},{4,6},{5,7},{6,4},{7,5},{8,10},{9,11},{10,... | collective-permute-start | bytes 3932168 | tf_op jit(solution)/shard_map/ppermute | solution.py:415
  128.2 311.5 %collective-permute-start.7 = (bf16[1,128,5120]{2,1,0:T(8,128)(2,1)}, bf16[1,128,5120]{2,1,0:T(8,128)(2,1)}, u32[]{:S(2)}, u32[]{:S(2)}) collective-permute-start(bf16[1,128,5120]{2,1,0:T(8,128)(2,1)} %get-tuple-element.44), channel_id=1, source_target_pairs={{0,3},{1,2},{2,1},{3,0},{4,7},{5,6},{6,5},{7,4},{8,11},{9,10},{10,... | collective-permute-start | bytes 3932168 | tf_op jit(solution)/shard_map/ppermute | solution.py:415
  437.3 109.0 %collective-permute-start.9 = (bf16[2,128,5120]{2,1,0:T(8,128)(2,1)}, bf16[2,128,5120]{2,1,0:T(8,128)(2,1)}, u32[]{:S(2)}, u32[]{:S(2)}) collective-permute-start(bf16[2,128,5120]{2,1,0:T(8,128)(2,1)} %get-tuple-element.48), channel_id=1, source_target_pairs={{0,3},{1,2},{2,1},{3,0},{4,7},{5,6},{6,5},{7,4},{8,11},{9,10},{10,... | collective-permute-start | bytes 7864328 | tf_op jit(solution)/shard_map/ppermute | solution.py:415
  438.9 114.0 %collective-permute-start.8 = (bf16[2,128,5120]{2,1,0:T(8,128)(2,1)}, bf16[2,128,5120]{2,1,0:T(8,128)(2,1)}, u32[]{:S(2)}, u32[]{:S(2)}) collective-permute-start(bf16[2,128,5120]{2,1,0:T(8,128)(2,1)} %get-tuple-element.45.refs_5_), channel_id=1, source_target_pairs={{0,2},{1,3},{2,0},{3,1},{4,6},{5,7},{6,4},{7,5},{8,10},{9,11},{10,... | collective-permute-start | bytes 7864328 | tf_op jit(solution)/shard_map/ppermute | solution.py:415
  607.6 60.2 %collective-permute-start.12 = (bf16[3,128,5120]{2,1,0:T(8,128)(2,1)}, bf16[3,128,5120]{2,1,0:T(8,128)(2,1)}, u32[]{:S(2)}, u32[]{:S(2)}) collective-permute-start(bf16[3,128,5120]{2,1,0:T(8,128)(2,1)} %get-tuple-element.52), channel_id=1, source_target_pairs={{0,1},{1,0},{2,3},{3,2},{4,5},{5,4},{6,7},{7,6},{8,9},{9,8},{10,11... | collective-permute-start | bytes 11796488 | tf_op jit(solution)/shard_map/ppermute | solution.py:415
  607.7 31.9 %collective-permute-start.10 = (bf16[1,128,5120]{2,1,0:T(8,128)(2,1)}, bf16[1,128,5120]{2,1,0:T(8,128)(2,1)S(1)}, u32[]{:S(2)}, u32[]{:S(2)}) collective-permute-start(bf16[1,128,5120]{2,1,0:T(8,128)(2,1)} %get-tuple-element.49.refs_8_), channel_id=1, source_target_pairs={{0,2},{1,3},{2,0},{3,1},{4,6},{5,7},{6,4},{7,5},{8,10},{9,11},{10,... | collective-permute-start | bytes 3932168 | tf_op jit(solution)/shard_map/ppermute | solution.py:415
  609.3 57.4 %collective-permute-start.11 = (bf16[1,128,5120]{2,1,0:T(8,128)(2,1)}, bf16[1,128,5120]{2,1,0:T(8,128)(2,1)S(1)}, u32[]{:S(2)}, u32[]{:S(2)}) collective-permute-start(bf16[1,128,5120]{2,1,0:T(8,128)(2,1)} %get-tuple-element.51), channel_id=1, source_target_pairs={{0,3},{1,2},{2,1},{3,0},{4,7},{5,6},{6,5},{7,4},{8,11},{9,10},{10,... | collective-permute-start | bytes 3932168 | tf_op jit(solution)/shard_map/ppermute | solution.py:415

commit v3 on v2

--- a/solution.py
+++ b/solution.py
@@ -24,10 +24,6 @@
     angles = pos_ids.astype(jnp.float32)[..., None] * inv_freq
     cos_t, sin_t = jnp.cos(angles), jnp.sin(angles)
     return cos_t, sin_t
-
-
-def pair_heads(gain):
-    return gain.reshape(-1, 2, 2, HEAD_DIM // 2).transpose(0, 2, 1, 3).reshape(1, -1)
 
 
 def lane_sums(sq):
@@ -73,14 +69,30 @@
     )(x_loc)
 
 
-def qkv_kernel(n_tiles, own, counts, aliased, *refs):
-    n_pieces = len(counts)
-    x_hbm = refs[:n_pieces]
-    weights = refs[n_pieces:n_pieces + 3]
-    qkv_out, stat_out, x_buf, w_buf, x_sem, w_sem = refs[n_pieces + 4 + 2 * aliased:]
+def qkv_kernel(n_tiles, n_arrays, takes, aliased, *refs):
+    arrays = refs[:n_arrays]
+    weights = refs[n_arrays:n_arrays + 3]
+    qkv_out, stat_out, x_buf, w_buf, o_buf, stat_buf, x_sem, w_sem, o_sem, stat_sem = refs[n_arrays + 4 + 2 * aliased:]
     step = pl.program_id(0)
-    rows = sum(counts) * 128
+    rows = x_buf.shape[0]
     slot = lax.rem(step, 2)
+    which = step // n_tiles
+    srcs, spots = [], []
+    for idx, own, first, count, rel, batch in takes:
+        base = lax.axis_index('sp') * count if own else first
+        srcs += [arrays[idx].at[base + b] for b in range(count)]
+        spots += [(rel, batch + b) for b in range(count)]
+
+    def result_copies(at_step):
+        cols = pl.ds(pl.multiple_of(lax.rem(at_step, n_tiles) * QKV_TILE, QKV_TILE), QKV_TILE)
+        frm = lax.rem(at_step, 2)
+        return [pltpu.make_async_copy(o_buf.at[frm, pl.ds(i * 128, 128), :], qkv_out.at[at_step // n_tiles, rel, b, :, cols],
+                                      o_sem.at[frm, i]) for i, (rel, b) in enumerate(spots)]
+
+    @pl.when(step >= 2)
+    def _():
+        for cp in result_copies(step - 2):
+            cp.wait()
 
     def fetch(at_step):
         for idx, w_ref in enumerate(weights):
@@ -92,10 +104,6 @@
 
     @pl.when(step == 0)
     def _():
-        srcs = []
-        for idx, (ref, count) in enumerate(zip(x_hbm, counts)):
-            base = lax.axis_index('sp') * count if own and idx == 0 else 0
-            srcs += [ref.at[base + b] for b in range(count)]
         copies = row_copies(srcs, x_buf, x_sem)
         for cp in copies:
             cp.start()
@@ -119,44 +127,54 @@
         even, odd = (proj[:, c].astype(jnp.bfloat16) for c in cols)
         moved = pltpu.roll(jnp.where(low, odd, even), 64, 1)
         for c, val in zip(cols, (jnp.where(keep_even, even, moved), jnp.where(keep_odd, odd, moved))):
-            qkv_out[0, :, :, :, c] = val.reshape(qkv_out.shape[1:4] + (128,))
+            o_buf[slot, :, c] = val
         even, odd = even.astype(jnp.float32), odd.astype(jnp.float32)
         sq = even * even + odd * odd
         part = sq if part is None else part + sq
-    part = part.reshape(stat_out.shape)
+    for cp in result_copies(step):
+        cp.start()
     first = lax.rem(step, n_tiles) == 0
 
     @pl.when(first)
     def _():
-        stat_out[...] = part
+        stat_buf[which] = part
 
     @pl.when(jnp.logical_not(first))
     def _():
-        stat_out[...] = stat_out[...] + part
-
-
-def qkv_call(pieces, counts, own, weights, per_dev, group, batch_block, prior, after):
+        stat_buf[which] = stat_buf[which] + part
+
+    @pl.when(step == 3 * n_tiles - 1)
+    def _():
+        copies = [pltpu.make_async_copy(stat_buf.at[w, pl.ds(i * 128, 128), :], stat_out.at[w, rel, b], stat_sem.at[w, i])
+                  for w in range(3) for i, (rel, b) in enumerate(spots)]
+        for cp in copies:
+            cp.start()
+        for cp in result_copies(step - 1) + result_copies(step) + copies:
+            cp.wait()
+
+
+def qkv_call(arrays, takes, weights, per_dev, prior, after):
     width = weights[0].shape[0]
     n_tiles = width // QKV_TILE
-    n_batch = sum(counts) // 2
-    rows = sum(counts) * 128
+    n_rows = sum(t[3] for t in takes)
+    rows = n_rows * 128
     any_spec = pl.BlockSpec(memory_space=pl.ANY)
-    n_in = len(pieces) + 4
+    n_in = len(arrays) + 4
     return pl.pallas_call(
-        functools.partial(qkv_kernel, n_tiles, own, counts, bool(prior)),
+        functools.partial(qkv_kernel, n_tiles, len(arrays), takes, bool(prior)),
         grid=(3 * n_tiles,),
         in_specs=[any_spec] * (n_in + len(prior)),
-        out_specs=[
-            pl.BlockSpec((1, 2, n_batch, 128, QKV_TILE), lambda s: (s // n_tiles, group, batch_block, 0, lax.rem(s, n_tiles))),
-            pl.BlockSpec((1, 2, n_batch, 128, 128), lambda s: (s // n_tiles, group, batch_block, 0, 0))],
+        out_specs=[any_spec] * 2,
         out_shape=[jax.ShapeDtypeStruct((3, 4, per_dev, 128, width), jnp.bfloat16),
                    jax.ShapeDtypeStruct((3, 4, per_dev, 128, 128), jnp.float32)],
         input_output_aliases={n_in: 0, n_in + 1: 1} if prior else {},
         scratch_shapes=[pltpu.VMEM((rows, width), jnp.bfloat16), pltpu.VMEM((2, width, QKV_TILE), jnp.bfloat16),
-                        pltpu.SemaphoreType.DMA((sum(counts),)), pltpu.SemaphoreType.DMA((2,))],
+                        pltpu.VMEM((2, rows, QKV_TILE), jnp.bfloat16), pltpu.VMEM((3, rows, 128), jnp.float32),
+                        pltpu.SemaphoreType.DMA((n_rows,)), pltpu.SemaphoreType.DMA((2,)),
+                        pltpu.SemaphoreType.DMA((2, n_rows)), pltpu.SemaphoreType.DMA((3, n_rows))],
         compiler_params=pltpu.CompilerParams(vmem_limit_bytes=VMEM_BYTES, dimension_semantics=("arbitrary",)),
         cost_estimate=pl.CostEstimate(flops=6 * rows * width * width, transcendentals=0, bytes_accessed=6 * width * width),
-    )(*pieces, *weights, after, *prior)
+    )(*arrays, *weights, after, *prior)
 
 
 def attention_kernel(width, dev_ref, *refs):
@@ -191,10 +209,12 @@
         sides = []
         for which, gain_ref in ((0, gq_ref), (1, gk_ref)):
             halves = []
+            even, odd = (gain_ref[:, pair * 256 + c:pair * 256 + c + 128].astype(jnp.float32) for c in (0, 128))
+            moved = pltpu.roll(jnp.where(low[:1], odd, even), 64, 1)
+            gains = jnp.where(low[:1], even, moved), jnp.where(low[:1], moved, odd)
             for half in range(2):
                 lanes = slice(pair * 256 + half * 128, pair * 256 + half * 128 + 128)
-                gain = gain_ref[:, lanes].astype(jnp.float32)
-                halves.append([qkv_refs[j][which, 0, 0, :, lanes].astype(jnp.float32) * gain for j in range(4)])
+                halves.append([qkv_refs[j][which, 0, 0, :, lanes].astype(jnp.float32) * gains[half] for j in range(4)])
             rot = ([], [])
             for j in range(4):
                 rows = slice(j * 128, (j + 1) * 128)
@@ -272,7 +292,7 @@
         compiler_params=pltpu.CompilerParams(vmem_limit_bytes=VMEM_BYTES, dimension_semantics=("arbitrary", "arbitrary")),
         cost_estimate=pl.CostEstimate(flops=n_batch * n_heads * 512 * 512 * 128 * 8, transcendentals=0,
                                       bytes_accessed=n_batch * 512 * width * 8),
-    )(dev, *[qkv] * 4, *[stats] * 4, cos_t, sin_t, pair_heads(gain_q), pair_heads(gain_k))
+    )(dev, *[qkv] * 4, *[stats] * 4, cos_t, sin_t, gain_q.reshape(1, width), gain_k.reshape(1, width))
 
 
 def out_kernel(n_tiles, rel, o_counts, x_counts, own, moved, *refs):
@@ -424,10 +444,10 @@
 
         weights = (w_query, w_key, w_value)
         dev_arr = jnp.full((1,), dev, jnp.int32)
-        near = qkv_call([x_loc, x_near], (per_dev, per_dev), True, weights, per_dev, 0, 0, (), gain_q)
+        near = qkv_call([x_loc, x_near], ((0, True, 0, per_dev, 0, 0), (1, False, 0, 2, 1, 0)), weights, per_dev, (), gain_q)
         p2, p3, x_far01[0], x_far01[1] = lax.optimization_barrier((p2, p3, x_far01[0], x_far01[1]))
         x_far2 = [swap(p2, 2), swap(p3, 3)]
-        qkv01, stats01 = qkv_call(x_far01, (2, 2), False, weights, per_dev, 1, 0, near, gain_q)
+        qkv01, stats01 = qkv_call(x_far01, ((0, False, 0, 2, 2, 0), (1, False, 0, 2, 3, 0)), weights, per_dev, near, gain_q)
         pos_parts, _ = lax.optimization_barrier((pos_parts, near[1]))
         pos_rel = jnp.stack(pos_parts)
         pos_mine = jnp.concatenate([lax.dynamic_index_in_dim(pos_rel, dev ^ j, axis=0, keepdims=False) for j in range(4)], axis=1)
@@ -435,7 +455,8 @@
         o01 = attention_call(qkv01, stats01, dev_arr, 0, 2, cos_t, sin_t, gain_q, gain_k)
         y_far01 = out_call([o01], (2, 3), x_far01, (2, 2), False, (2, 2), w_out, gain_out, gain_q)
         z_far01 = [swap(y_far01[0], 2), swap(y_far01[1], 3)]
-        qkv2, stats2 = qkv_call(x_far2, (1, 1), False, weights, per_dev, 1, 2, (qkv01, stats01), y_far01[0])
+        qkv2, stats2 = qkv_call([x_near] + x_far2, ((0, False, 2, 1, 1, 2), (1, False, 0, 1, 2, 2), (2, False, 0, 1, 3, 2)), weights, per_dev,
+                                 (qkv01, stats01), y_far01[0])
         o2 = attention_call(qkv2, stats2, dev_arr, 2, 1, cos_t, sin_t, gain_q, gain_k)
         y_far2 = out_call([o2], (2, 3), x_far2, (1, 1), False, (1, 1), w_out, gain_out, gain_q)
         z_far2 = [swap(y_far2[0], 2), swap(y_far2[1], 3)]

time: 673 us -> 662 us (0.984)
    pallas_call x3, Pallas kernels: 287 us -> 280 us  [qkv_call(): pl.pallas_call(functools.partial(qkv_kernel, n_tiles, len(arrays), takes,...]
  transfers between devices with their start and end apart: 13 -> 13, of which waited for: 5 -> 4; matrix products, arithmetic and copies ran while one was open for 1% -> 1% of each run, Pallas kernels for 62% -> 62%
where the time goes in v3:
time: 662 us; the launch traced here: 661 us
  Pallas kernels  471 us (71%)
  waiting for transfers between devices  164 us (25%)
  starting transfers between devices  13.1 us (2%)
  local copies, waits for them, and re-layouts  8.47 us (1%)
    pallas_call x3, Pallas kernels, qkv_call(): pl.pallas_call(functools.partial(qkv_kernel, n_tiles, len(arrays), takes,...  280 us
    ppermute x13, waiting for transfers between devices, swap(): return lax.ppermute(arr, 'sp', [(i, i ^ r) for i in range(4)])  164 us
    pallas_call x3, Pallas kernels, out_call(): pl.pallas_call(functools.partial(out_kernel, n_tiles, rel, o_counts, x_co...  122 us
    pallas_call x2, Pallas kernels, attention_call(): pl.pallas_call(functools.partial(attention_kernel, width), grid_spec=pltp...  59.4 us
  transfers between devices with their start and end apart: 13, of which 4 were waited for; matrix products, arithmetic and copies ran while one was open for 1% of the time, Pallas kernels for 62%

profile of v3, /device:TPU:0, one launch (start us, length us, event | category | flops | bytes accessed | tf_op | source)
XLA Modules:
  0.0 661.0 jit_solution(2568061107952958834)
XLA Ops:
  0.0 3.3 shard_map.92
  3.3 0.0 copy-start.3
  3.3 0.0 copy-start.1
  3.3 0.0 copy-start.2
  3.3 0.0 copy-start
  3.3 0.8 collective-permute-start.2
  4.1 6.3 shard_map.91
  10.4 2.5 collective-permute-start
  13.0 0.1 collective-permute-start.1
  13.1 0.0 copy-done.3
  13.1 1.6 collective-permute-start.5
  14.8 0.2 collective-permute-start.3
  15.0 0.0 copy-done.1
  15.0 0.6 reshape.54.refs_4_.refs_7_
  15.6 0.0 copy-done.2
  15.6 0.6 reshape.53.refs_11_
  16.2 0.0 copy-done
  16.2 0.6 reshape.52.refs_10_
  16.8 54.2 %collective-permute-done.refs_0_.refs_1_ = bf16[2,128,5120]{2,1,0:T(8,128)(2,1)} collective-permute-done((bf16[2,128,5120]{2,1,0:T(8,128)(2,1)}, bf16[2,128,5120]{2,1,0:T(8,128)(2,1)}, u32[]{:S(2)}, u32[]{:S(2)}) %collective-permute-start) | collective-permute-done | bytes 2621472 | tf_op jit(solution)/shard_map/ppermute | solution.py:435
  71.0 2.0 collective-permute-start.4
  73.0 53.7 %collective-permute-done.1.refs_1_.refs_2_ = bf16[2,128,5120]{2,1,0:T(8,128)(2,1)} collective-permute-done((bf16[2,128,5120]{2,1,0:T(8,128)(2,1)}, bf16[2,128,5120]{2,1,0:T(8,128)(2,1)}, u32[]{:S(2)}, u32[]{:S(2)}) %collective-permute-start.1) | collective-permute-done | bytes 2621472 | tf_op jit(solution)/shard_map/ppermute | solution.py:435
  126.8 1.5 collective-permute-start.6
  128.2 0.0 collective-permute-done.2.refs_1_.refs_0_.refs_3_
  128.2 0.0 collective-permute-start.7
  128.2 114.7 %shard_map.93 = (bf16[3,4,3,128,5120]{4,3,2,1,0:T(8,128)(2,1)}, f32[3,4,3,128,128]{4,3,2,1,0:T(8,128)}) custom-call(bf16[12,128,5120]{2,1,0:T(8,128)(2,1)} %refs_2_.5, bf16[3,128,5120]{2,1,0:T(8,128)(2,1)} %collective-permute-done.2.refs_1_.refs_0_.refs_3_, bf16[5120,5120]{1,0:T(8,128)(2,1)} %refs_3_.8, bf16[5120,5120]{1,0:T(8,128)(2,1)} %refs_4_.5, ...), custom_call_target="tpu_custom_call" | custom-call | flops 100663296000 | bytes 157286400 | tf_op jit(solution)/shard_map/pallas_call | solution.py:163
  242.9 0.0 collective-permute-done.5
  242.9 0.0 collective-permute-done.3
  243.0 0.0 collective-permute-done.4
  243.0 4.3 multiply_sine_fusion
  247.4 93.5 %shard_map.94 = (bf16[3,4,3,128,5120]{4,3,2,1,0:T(8,128)(2,1)}, f32[3,4,3,128,128]{4,3,2,1,0:T(8,128)}) custom-call(bf16[2,128,5120]{2,1,0:T(8,128)(2,1)} %collective-permute-done.refs_0_.refs_1_, bf16[2,128,5120]{2,1,0:T(8,128)(2,1)} %collective-permute-done.1.refs_1_.refs_2_, ...), custom_call_target="tpu_custom_call", output_to_operand_aliasing={{0}: (6, {}), {1}: (7, {})} | custom-call | flops 80530636800 | bytes 157286400 | tf_op jit(solution)/shard_map/pallas_call | solution.py:163
  340.8 39.2 %shard_map.95.refs_0_ = bf16[4,2,128,5120]{3,2,1,0:T(8,128)(2,1)} custom-call(s32[1]{0:T(128)} %bitcast.dev_ref, bf16[3,4,3,128,5120]{4,3,2,1,0:T(8,128)(2,1)} %get-tuple-element.37.refs_0_.refs_1_.refs_2_.refs_3_.refs_7_, bf16[3,4,3,128,5120]{4,3,2,1,0:T(8,128)(2,1)} %get-tuple-element.37.refs_0_.refs_1_.refs_2_.refs_3_.refs_7_, ...), custom_call_target="tpu_custom_call" | custom-call | flops 21474836480 | bytes 41943040 | tf_op jit(solution)/shard_map/pallas_call | solution.py:281
  380.0 39.1 %shard_map.96 = (bf16[2,128,5120]{2,1,0:T(8,128)(2,1)}, bf16[2,128,5120]{2,1,0:T(8,128)(2,1)}) custom-call(bf16[4,2,128,5120]{3,2,1,0:T(8,128)(2,1)} %shard_map.95.refs_0_, bf16[2,128,5120]{2,1,0:T(8,128)(2,1)} %collective-permute-done.refs_0_.refs_1_, bf16[2,128,5120]{2,1,0:T(8,128)(2,1)} %collective-permute-done.1.refs_1_.refs_2_, ...), custom_call_target="tpu_custom_call" | custom-call | flops 26843545600 | bytes 52428800 | tf_op jit(solution)/shard_map/pallas_call | solution.py:412
  419.0 1.7 collective-permute-start.9
  420.7 0.7 collective-permute-start.8
  421.5 0.0 collective-permute-done.6.refs_1_
  421.5 0.0 collective-permute-done.7.refs_2_
  421.5 72.1 %shard_map.97 = (bf16[3,4,3,128,5120]{4,3,2,1,0:T(8,128)(2,1)}, f32[3,4,3,128,128]{4,3,2,1,0:T(8,128)}) custom-call(bf16[3,128,5120]{2,1,0:T(8,128)(2,1)} %collective-permute-done.2.refs_1_.refs_0_.refs_3_, bf16[1,128,5120]{2,1,0:T(8,128)(2,1)} %collective-permute-done.6.refs_1_, ...), custom_call_target="tpu_custom_call", output_to_operand_aliasing={{0}: (7, {}), {1}: (8, {})} | custom-call | flops 60397977600 | bytes 157286400 | tf_op jit(solution)/shard_map/pallas_call | solution.py:163
  493.6 20.2 %shard_map.98.refs_0_.refs_1_ = bf16[4,1,128,5120]{3,2,1,0:T(8,128)(2,1)} custom-call(s32[1]{0:T(128)} %bitcast.dev_ref, bf16[3,4,3,128,5120]{4,3,2,1,0:T(8,128)(2,1)} %get-tuple-element.46.refs_0_.refs_1_.refs_2_.refs_3_, bf16[3,4,3,128,5120]{4,3,2,1,0:T(8,128)(2,1)} %get-tuple-element.46.refs_0_.refs_1_.refs_2_.refs_3_, ...), custom_call_target="tpu_custom_call" | custom-call | flops 10737418240 | bytes 20971520 | tf_op jit(solution)/shard_map/pallas_call | solution.py:281
  513.8 28.0 %shard_map.99 = (bf16[1,128,5120]{2,1,0:T(8,128)(2,1)}, bf16[1,128,5120]{2,1,0:T(8,128)(2,1)}) custom-call(bf16[4,1,128,5120]{3,2,1,0:T(8,128)(2,1)} %shard_map.98.refs_0_.refs_1_, bf16[1,128,5120]{2,1,0:T(8,128)(2,1)} %collective-permute-done.6.refs_1_, bf16[1,128,5120]{2,1,0:T(8,128)(2,1)} %collective-permute-done.7.refs_2_, bf16[5120,5120]{1,0:T(8,128)(2,1)} %refs_6_.1, ...), custom_call_target="tpu_custom_call" | custom-call | flops 13421772800 | bytes 52428800 | tf_op jit(solution)/shard_map/pallas_call | solution.py:412
  541.8 0.0 collective-permute-done.9.refs_5_
  541.8 0.0 collective-permute-done.8.refs_4_
  541.8 54.7 %shard_map.100 = (bf16[12,128,5120]{2,1,0:T(8,128)(2,1)}, bf16[3,128,5120]{2,1,0:T(8,128)(2,1)}) custom-call(bf16[4,2,128,5120]{3,2,1,0:T(8,128)(2,1)} %shard_map.95.refs_0_, bf16[4,1,128,5120]{3,2,1,0:T(8,128)(2,1)} %shard_map.98.refs_0_.refs_1_, bf16[12,128,5120]{2,1,0:T(8,128)(2,1)} %refs_2_.5, ...), custom_call_target="tpu_custom_call" | custom-call | flops 40265318400 | bytes 52428800 | tf_op jit(solution)/shard_map/pallas_call | solution.py:412
  596.5 0.0 collective-permute-start.12
  596.6 1.3 collective-permute-start.10
  597.8 0.6 collective-permute-start.11
  598.4 30.0 %collective-permute-done.10 = bf16[1,128,5120]{2,1,0:T(8,128)(2,1)S(1)} collective-permute-done((bf16[1,128,5120]{2,1,0:T(8,128)(2,1)}, bf16[1,128,5120]{2,1,0:T(8,128)(2,1)S(1)}, u32[]{:S(2)}, u32[]{:S(2)}) %collective-permute-start.10) | collective-permute-done | bytes 1310752 | tf_op jit(solution)/shard_map/ppermute | solution.py:435
  628.5 1.1 constant_dynamic-update-slice_fusion.2
  629.6 25.9 %collective-permute-done.11 = bf16[1,128,5120]{2,1,0:T(8,128)(2,1)S(1)} collective-permute-done((bf16[1,128,5120]{2,1,0:T(8,128)(2,1)}, bf16[1,128,5120]{2,1,0:T(8,128)(2,1)S(1)}, u32[]{:S(2)}, u32[]{:S(2)}) %collective-permute-start.11) | collective-permute-done | bytes 1310752 | tf_op jit(solution)/shard_map/ppermute | solution.py:435
  655.5 1.1 constant_dynamic-update-slice_fusion.1
  656.7 0.0 collective-permute-done.12
  656.7 4.3 constant_dynamic-update-slice_fusion
  (5 shorter events, 0.1 us)
Async XLA Ops:
  3.3 9.8 %copy-start.3 = (s32[12,128]{1,0:T(8,128)S(1)}, s32[12,128]{1,0:T(8,128)}, u32[]{:S(2)}) copy-start(s32[12,128]{1,0:T(8,128)} %param.10) | copy-start | bytes 18436
  3.3 11.7 %copy-start.1 = (bf16[5120]{0:T(1024)(128)(2,1)S(1)}, bf16[5120]{0:T(1024)(128)(2,1)}, u32[]{:S(2)}) copy-start(bf16[5120]{0:T(1024)(128)(2,1)} %param.17) | copy-start | bytes 30724
  3.3 12.3 %copy-start.2 = (bf16[5120]{0:T(1024)(128)(2,1)S(1)}, bf16[5120]{0:T(1024)(128)(2,1)}, u32[]{:S(2)}) copy-start(bf16[5120]{0:T(1024)(128)(2,1)} %param.16) | copy-start | bytes 30724
  3.3 12.9 %copy-start = (bf16[5120]{0:T(1024)(128)(2,1)S(1)}, bf16[5120]{0:T(1024)(128)(2,1)}, u32[]{:S(2)}) copy-start(bf16[5120]{0:T(1024)(128)(2,1)} %refs_5_.9) | copy-start | bytes 30724
  3.3 124.9 %collective-permute-start.2 = (bf16[3,128,5120]{2,1,0:T(8,128)(2,1)}, bf16[3,128,5120]{2,1,0:T(8,128)(2,1)}, u32[]{:S(2)}, u32[]{:S(2)}) collective-permute-start(bf16[3,128,5120]{2,1,0:T(8,128)(2,1)} %shard_map.92), channel_id=1, source_target_pairs={{0,1},{1,0},{2,3},{3,2},{4,5},{5,4},{6,7},{7,6},{8,9},{9,8},{10,11... | collective-permute-start | bytes 11796488 | tf_op jit(solution)/shard_map/ppermute | solution.py:435
  10.4 60.6 %collective-permute-start = (bf16[2,128,5120]{2,1,0:T(8,128)(2,1)}, bf16[2,128,5120]{2,1,0:T(8,128)(2,1)}, u32[]{:S(2)}, u32[]{:S(2)}) collective-permute-start(bf16[2,128,5120]{2,1,0:T(8,128)(2,1)} %get-tuple-element.31), channel_id=1, source_target_pairs={{0,2},{1,3},{2,0},{3,1},{4,6},{5,7},{6,4},{7,5},{8,10},{9,11},{10,... | collective-permute-start | bytes 7864328 | tf_op jit(solution)/shard_map/ppermute | solution.py:435
  13.0 113.8 %collective-permute-start.1 = (bf16[2,128,5120]{2,1,0:T(8,128)(2,1)}, bf16[2,128,5120]{2,1,0:T(8,128)(2,1)}, u32[]{:S(2)}, u32[]{:S(2)}) collective-permute-start(bf16[2,128,5120]{2,1,0:T(8,128)(2,1)} %get-tuple-element.32), channel_id=1, source_target_pairs={{0,3},{1,2},{2,1},{3,0},{4,7},{5,6},{6,5},{7,4},{8,11},{9,10},{10,... | collective-permute-start | bytes 7864328 | tf_op jit(solution)/shard_map/ppermute | solution.py:435
  13.1 229.8 %collective-permute-start.5 = (s32[3,128]{1,0:T(4,128)S(1)}, s32[3,128]{1,0:T(4,128)S(1)}, u32[]{:S(2)}, u32[]{:S(2)}) collective-permute-start(s32[3,128]{1,0:T(4,128)S(1)} %get-tuple-element.59), channel_id=1, source_target_pairs={{0,3},{1,2},{2,1},{3,0},{4,7},{5,6},{6,5},{7,4},{8,11},{9,10},{10,... | collective-permute-start | bytes 4616 | tf_op jit(solution)/shard_map/ppermute | solution.py:435
  14.8 228.2 %collective-permute-start.3 = (s32[3,128]{1,0:T(4,128)S(1)}, s32[3,128]{1,0:T(4,128)S(1)}, u32[]{:S(2)}, u32[]{:S(2)}) collective-permute-start(s32[3,128]{1,0:T(4,128)S(1)} %get-tuple-element.60), channel_id=1, source_target_pairs={{0,1},{1,0},{2,3},{3,2},{4,5},{5,4},{6,7},{7,6},{8,9},{9,8},{10,11... | collective-permute-start | bytes 4616 | tf_op jit(solution)/shard_map/ppermute | solution.py:435
  71.0 171.9 %collective-permute-start.4 = (s32[3,128]{1,0:T(4,128)S(1)}, s32[3,128]{1,0:T(4,128)S(1)}, u32[]{:S(2)}, u32[]{:S(2)}) collective-permute-start(s32[3,128]{1,0:T(4,128)S(1)} %get-tuple-element.62), channel_id=1, source_target_pairs={{0,2},{1,3},{2,0},{3,1},{4,6},{5,7},{6,4},{7,5},{8,10},{9,11},{10,... | collective-permute-start | bytes 4616 | tf_op jit(solution)/shard_map/ppermute | solution.py:435
  126.8 294.7 %collective-permute-start.6 = (bf16[1,128,5120]{2,1,0:T(8,128)(2,1)}, bf16[1,128,5120]{2,1,0:T(8,128)(2,1)}, u32[]{:S(2)}, u32[]{:S(2)}) collective-permute-start(bf16[1,128,5120]{2,1,0:T(8,128)(2,1)} %get-tuple-element.43), channel_id=1, source_target_pairs={{0,2},{1,3},{2,0},{3,1},{4,6},{5,7},{6,4},{7,5},{8,10},{9,11},{10,... | collective-permute-start | bytes 3932168 | tf_op jit(solution)/shard_map/ppermute | solution.py:435
  128.2 293.2 %collective-permute-start.7 = (bf16[1,128,5120]{2,1,0:T(8,128)(2,1)}, bf16[1,128,5120]{2,1,0:T(8,128)(2,1)}, u32[]{:S(2)}, u32[]{:S(2)}) collective-permute-start(bf16[1,128,5120]{2,1,0:T(8,128)(2,1)} %get-tuple-element.44), channel_id=1, source_target_pairs={{0,3},{1,2},{2,1},{3,0},{4,7},{5,6},{6,5},{7,4},{8,11},{9,10},{10,... | collective-permute-start | bytes 3932168 | tf_op jit(solution)/shard_map/ppermute | solution.py:435
  419.0 122.8 %collective-permute-start.9 = (bf16[2,128,5120]{2,1,0:T(8,128)(2,1)}, bf16[2,128,5120]{2,1,0:T(8,128)(2,1)}, u32[]{:S(2)}, u32[]{:S(2)}) collective-permute-start(bf16[2,128,5120]{2,1,0:T(8,128)(2,1)} %get-tuple-element.48), channel_id=1, source_target_pairs={{0,3},{1,2},{2,1},{3,0},{4,7},{5,6},{6,5},{7,4},{8,11},{9,10},{10,... | collective-permute-start | bytes 7864328 | tf_op jit(solution)/shard_map/ppermute | solution.py:435
  420.7 121.1 %collective-permute-start.8 = (bf16[2,128,5120]{2,1,0:T(8,128)(2,1)}, bf16[2,128,5120]{2,1,0:T(8,128)(2,1)}, u32[]{:S(2)}, u32[]{:S(2)}) collective-permute-start(bf16[2,128,5120]{2,1,0:T(8,128)(2,1)} %get-tuple-element.45.refs_6_), channel_id=1, source_target_pairs={{0,2},{1,3},{2,0},{3,1},{4,6},{5,7},{6,4},{7,5},{8,10},{9,11},{10,... | collective-permute-start | bytes 7864328 | tf_op jit(solution)/shard_map/ppermute | solution.py:435
  596.5 60.2 %collective-permute-start.12 = (bf16[3,128,5120]{2,1,0:T(8,128)(2,1)}, bf16[3,128,5120]{2,1,0:T(8,128)(2,1)}, u32[]{:S(2)}, u32[]{:S(2)}) collective-permute-start(bf16[3,128,5120]{2,1,0:T(8,128)(2,1)} %get-tuple-element.52), channel_id=1, source_target_pairs={{0,1},{1,0},{2,3},{3,2},{4,5},{5,4},{6,7},{7,6},{8,9},{9,8},{10,11... | collective-permute-start | bytes 11796488 | tf_op jit(solution)/shard_map/ppermute | solution.py:435
  596.6 31.9 %collective-permute-start.10 = (bf16[1,128,5120]{2,1,0:T(8,128)(2,1)}, bf16[1,128,5120]{2,1,0:T(8,128)(2,1)S(1)}, u32[]{:S(2)}, u32[]{:S(2)}) collective-permute-start(bf16[1,128,5120]{2,1,0:T(8,128)(2,1)} %get-tuple-element.49.refs_8_), channel_id=1, source_target_pairs={{0,2},{1,3},{2,0},{3,1},{4,6},{5,7},{6,4},{7,5},{8,10},{9,11},{10,... | collective-permute-start | bytes 3932168 | tf_op jit(solution)/shard_map/ppermute | solution.py:435
  597.8 57.7 %collective-permute-start.11 = (bf16[1,128,5120]{2,1,0:T(8,128)(2,1)}, bf16[1,128,5120]{2,1,0:T(8,128)(2,1)S(1)}, u32[]{:S(2)}, u32[]{:S(2)}) collective-permute-start(bf16[1,128,5120]{2,1,0:T(8,128)(2,1)} %get-tuple-element.51), channel_id=1, source_target_pairs={{0,3},{1,2},{2,1},{3,0},{4,7},{5,6},{6,5},{7,4},{8,11},{9,10},{10,... | collective-permute-start | bytes 3932168 | tf_op jit(solution)/shard_map/ppermute | solution.py:435
